TPU v7x, 128 devices: a whole 4x4x4 slice. The times are simulated.
128 devices in a mesh: dp: 1, cols: 64 (over z, y, x), rows: 2 (over core).
Axes of the slice: x: 4, y: 4, z: 4, core: 2. Of those that a mesh axis runs over, the one named last changes fastest.
Arguments:
- h_init: bfloat16 [1, 48, 4096, 192], P('dp', 'rows', 'cols')
- c_init: float32 [1, 48, 4096, 192], P('dp', 'rows', 'cols')
- w_rec: bfloat16 [3, 3, 192, 768], replicated
- gate_bias: float32 [16, 768], replicated
Outputs:
- output 1: bfloat16 [16, 1, 48, 4096, 192], P(None, 'dp', 'rows', 'cols')
- output 2: float32 [1, 48, 4096, 192], P('dp', 'rows', 'cols')
All inputs are finite; a program needn't handle non-finite values.
Results may differ from a plain program's by a relative error of at most 0.00320178.
Values are sent between devices in bfloat16 or wider.
A program may use at most 1 GiB of HBM per device.

v0:
```python
import jax
import jax.numpy as jnp
from jax import lax
from jax.sharding import PartitionSpec as P


def lstm_update(gate_pre, c_prev):
    in_gate, forget_gate, out_gate, cand_gate = jnp.split(gate_pre, 4, axis=-1)
    c_next = jax.nn.sigmoid(forget_gate) * c_prev + jax.nn.sigmoid(in_gate) * jnp.tanh(cand_gate)
    h_next = (jax.nn.sigmoid(out_gate) * jnp.tanh(c_next)).astype(jnp.bfloat16)
    return h_next, c_next


def solution(mesh):
    row_count = mesh.shape["rows"]
    col_count = mesh.shape["cols"]
    rows_down = [(src_pos, src_pos + 1) for src_pos in range(row_count - 1)]
    rows_up = [(src_pos + 1, src_pos) for src_pos in range(row_count - 1)]
    cols_right = [(src_pos, src_pos + 1) for src_pos in range(col_count - 1)]
    cols_left = [(src_pos + 1, src_pos) for src_pos in range(col_count - 1)]

    def with_halo(tile):
        from_above = lax.ppermute(tile[:, -1:], "rows", rows_down)
        from_below = lax.ppermute(tile[:, :1], "rows", rows_up)
        tall_tile = jnp.concatenate([from_above, tile, from_below], axis=1)
        from_left = lax.ppermute(tall_tile[:, :, -1:], "cols", cols_right)
        from_right = lax.ppermute(tall_tile[:, :, :1], "cols", cols_left)
        return jnp.concatenate([from_left, tall_tile, from_right], axis=2)

    def device_fn(h_init, c_init, w_rec, gate_bias):
        def one_step(carry_in, bias_row):
            h_prev, c_prev = carry_in
            padded = with_halo(h_prev)
            gate_pre = lax.conv_general_dilated(padded, w_rec, (1, 1), "VALID", dimension_numbers=("NHWC", "HWIO", "NHWC"), preferred_element_type=jnp.float32) + bias_row
            h_next, c_next = lstm_update(gate_pre, c_prev)
            return (h_next, c_next), h_next

        final_state, h_seq = lax.scan(one_step, (h_init, c_init), gate_bias)
        return h_seq, final_state[1]

    state_spec = P("dp", "rows", "cols", None)
    return jax.shard_map(device_fn, mesh=mesh, in_specs=(state_spec, state_spec, P(), P()), out_specs=(P(None, "dp", "rows", "cols", None), state_spec), check_vma=False)
```

profile of v0, /device:TPU:97, one launch (start us, length us, event | category | flops | bytes accessed | tf_op | source)
XLA Modules:
  0.0 494.1 jit_solution(1255811974216978864)
XLA Ops:
  3.3 489.2 %while.14 = (s32[]{:T(128)}, bf16[1,24,64,192]{3,1,2,0:T(8,128)(2,1)S(1)}, f32[1,24,64,192]{3,1,2,0:T(8,128)S(1)}, bf16[16,1,24,64,192]{4,3,2,1,0:T(8,128)(2,1)}...) while((s32[]{:T(128)}, ...), condition=%wide.region_1.2_spmd, body=%wide.region_0.1_spmd.sunk | while | flops 4599613440 | bytes 50010996 | solution.py:38
  9.2 6.7 %collective-permute-start.2 = (bf16[1,26,1,192]{3,1,2,0:T(8,128)(2,1)S(1)}, bf16[1,26,1,192]{3,1,2,0:T(8,128)(2,1)S(1)}, u32[]{:S(2)}, u32[]{:S(2)}) collective-permute-start(bf16[1,26,1,192]{3,1,2,0:T(8,128)(2,1)S(1)} %get-tuple-element.114), channel_id=1, source_target_pairs={{2,0},{4,2},{6,4},{8,6},{10,8},{12,10},{14,12},{16,14},{18,16},{20... | collective-permute-start | bytes 29960 | tf_op jit(solution)/shard_map/while/body/eval_jaxpr/ppermute | solution.py:27
  18.6 6.0 %collective-permute-done.3 = bf16[1,26,1,192]{3,1,2,0:T(8,128)(2,1)S(1)} collective-permute-done((bf16[1,26,1,192]{3,1,2,0:T(8,128)(2,1)S(1)}, bf16[1,26,1,192]{3,1,2,0:T(8,128)(2,1)S(1)}, u32[]{:S(2)}, u32[]{:S(2)}) %collective-permute-start.3) | collective-permute-done | bytes 10016 | tf_op jit(solution)/shard_map/while/body/eval_jaxpr/ppermute | solution.py:26
  27.0 5.4 %select_add_fusion.2 = f32[24,8,9,768]{3,1,2,0:T(8,128)S(1)} fusion(f32[768]{0:T(1024)S(1)} %dynamic-slice_reduce_fusion.2, pred[8,9]{0,1:T(8,128)(4,1)S(1)} %get-tuple-element.146, bf16[3,3,192,768]{3,2,1,0:T(8,128)(2,1)S(1)} %copy-done.1, bf16[26,1,7,2,192]{4,2,3,0,1:T(8,128)(2,1)S(1)} %slice.80, bf16[26,1,8,9,192]{4,2,3,0,1:T(8,128)(2,1)S(1)} %copy.24), kind=kOutput, calls=%fused_computation.clone.1 | convolution fusion | flops 4591761408 | bytes 8824392 | tf_op jit(solution)/shard_map/while/body/eval_jaxpr/conv_general_dilated | solution.py:34
  50.6 4.6 collective-permute-done.3
  57.6 5.4 %select_add_fusion.2 = f32[24,8,9,768]{3,1,2,0:T(8,128)S(1)} fusion(f32[768]{0:T(1024)S(1)} %dynamic-slice_reduce_fusion.2, pred[8,9]{0,1:T(8,128)(4,1)S(1)} %get-tuple-element.146, bf16[3,3,192,768]{3,2,1,0:T(8,128)(2,1)S(1)} %copy-done.1, bf16[26,1,7,2,192]{4,2,3,0,1:T(8,128)(2,1)S(1)} %slice.80, bf16[26,1,8,9,192]{4,2,3,0,1:T(8,128)(2,1)S(1)} %copy.24), kind=kOutput, calls=%fused_computation.clone.1 | convolution fusion | flops 4591761408 | bytes 8824392 | tf_op jit(solution)/shard_map/while/body/eval_jaxpr/conv_general_dilated | solution.py:34
  80.9 4.6 collective-permute-done.3
  87.9 5.4 %select_add_fusion.2 = f32[24,8,9,768]{3,1,2,0:T(8,128)S(1)} fusion(f32[768]{0:T(1024)S(1)} %dynamic-slice_reduce_fusion.2, pred[8,9]{0,1:T(8,128)(4,1)S(1)} %get-tuple-element.146, bf16[3,3,192,768]{3,2,1,0:T(8,128)(2,1)S(1)} %copy-done.1, bf16[26,1,7,2,192]{4,2,3,0,1:T(8,128)(2,1)S(1)} %slice.80, bf16[26,1,8,9,192]{4,2,3,0,1:T(8,128)(2,1)S(1)} %copy.24), kind=kOutput, calls=%fused_computation.clone.1 | convolution fusion | flops 4591761408 | bytes 8824392 | tf_op jit(solution)/shard_map/while/body/eval_jaxpr/conv_general_dilated | solution.py:34
  111.2 4.6 collective-permute-done.3
  118.2 5.4 %select_add_fusion.2 = f32[24,8,9,768]{3,1,2,0:T(8,128)S(1)} fusion(f32[768]{0:T(1024)S(1)} %dynamic-slice_reduce_fusion.2, pred[8,9]{0,1:T(8,128)(4,1)S(1)} %get-tuple-element.146, bf16[3,3,192,768]{3,2,1,0:T(8,128)(2,1)S(1)} %copy-done.1, bf16[26,1,7,2,192]{4,2,3,0,1:T(8,128)(2,1)S(1)} %slice.80, bf16[26,1,8,9,192]{4,2,3,0,1:T(8,128)(2,1)S(1)} %copy.24), kind=kOutput, calls=%fused_computation.clone.1 | convolution fusion | flops 4591761408 | bytes 8824392 | tf_op jit(solution)/shard_map/while/body/eval_jaxpr/conv_general_dilated | solution.py:34
  141.5 4.6 collective-permute-done.3
  148.4 5.4 %select_add_fusion.2 = f32[24,8,9,768]{3,1,2,0:T(8,128)S(1)} fusion(f32[768]{0:T(1024)S(1)} %dynamic-slice_reduce_fusion.2, pred[8,9]{0,1:T(8,128)(4,1)S(1)} %get-tuple-element.146, bf16[3,3,192,768]{3,2,1,0:T(8,128)(2,1)S(1)} %copy-done.1, bf16[26,1,7,2,192]{4,2,3,0,1:T(8,128)(2,1)S(1)} %slice.80, bf16[26,1,8,9,192]{4,2,3,0,1:T(8,128)(2,1)S(1)} %copy.24), kind=kOutput, calls=%fused_computation.clone.1 | convolution fusion | flops 4591761408 | bytes 8824392 | tf_op jit(solution)/shard_map/while/body/eval_jaxpr/conv_general_dilated | solution.py:34
  171.8 4.6 collective-permute-done.3
  178.7 5.4 %select_add_fusion.2 = f32[24,8,9,768]{3,1,2,0:T(8,128)S(1)} fusion(f32[768]{0:T(1024)S(1)} %dynamic-slice_reduce_fusion.2, pred[8,9]{0,1:T(8,128)(4,1)S(1)} %get-tuple-element.146, bf16[3,3,192,768]{3,2,1,0:T(8,128)(2,1)S(1)} %copy-done.1, bf16[26,1,7,2,192]{4,2,3,0,1:T(8,128)(2,1)S(1)} %slice.80, bf16[26,1,8,9,192]{4,2,3,0,1:T(8,128)(2,1)S(1)} %copy.24), kind=kOutput, calls=%fused_computation.clone.1 | convolution fusion | flops 4591761408 | bytes 8824392 | tf_op jit(solution)/shard_map/while/body/eval_jaxpr/conv_general_dilated | solution.py:34
  209.0 5.4 %select_add_fusion.2 = f32[24,8,9,768]{3,1,2,0:T(8,128)S(1)} fusion(f32[768]{0:T(1024)S(1)} %dynamic-slice_reduce_fusion.2, pred[8,9]{0,1:T(8,128)(4,1)S(1)} %get-tuple-element.146, bf16[3,3,192,768]{3,2,1,0:T(8,128)(2,1)S(1)} %copy-done.1, bf16[26,1,7,2,192]{4,2,3,0,1:T(8,128)(2,1)S(1)} %slice.80, bf16[26,1,8,9,192]{4,2,3,0,1:T(8,128)(2,1)S(1)} %copy.24), kind=kOutput, calls=%fused_computation.clone.1 | convolution fusion | flops 4591761408 | bytes 8824392 | tf_op jit(solution)/shard_map/while/body/eval_jaxpr/conv_general_dilated | solution.py:34
  239.3 5.4 %select_add_fusion.2 = f32[24,8,9,768]{3,1,2,0:T(8,128)S(1)} fusion(f32[768]{0:T(1024)S(1)} %dynamic-slice_reduce_fusion.2, pred[8,9]{0,1:T(8,128)(4,1)S(1)} %get-tuple-element.146, bf16[3,3,192,768]{3,2,1,0:T(8,128)(2,1)S(1)} %copy-done.1, bf16[26,1,7,2,192]{4,2,3,0,1:T(8,128)(2,1)S(1)} %slice.80, bf16[26,1,8,9,192]{4,2,3,0,1:T(8,128)(2,1)S(1)} %copy.24), kind=kOutput, calls=%fused_computation.clone.1 | convolution fusion | flops 4591761408 | bytes 8824392 | tf_op jit(solution)/shard_map/while/body/eval_jaxpr/conv_general_dilated | solution.py:34
  269.6 5.4 %select_add_fusion.2 = f32[24,8,9,768]{3,1,2,0:T(8,128)S(1)} fusion(f32[768]{0:T(1024)S(1)} %dynamic-slice_reduce_fusion.2, pred[8,9]{0,1:T(8,128)(4,1)S(1)} %get-tuple-element.146, bf16[3,3,192,768]{3,2,1,0:T(8,128)(2,1)S(1)} %copy-done.1, bf16[26,1,7,2,192]{4,2,3,0,1:T(8,128)(2,1)S(1)} %slice.80, bf16[26,1,8,9,192]{4,2,3,0,1:T(8,128)(2,1)S(1)} %copy.24), kind=kOutput, calls=%fused_computation.clone.1 | convolution fusion | flops 4591761408 | bytes 8824392 | tf_op jit(solution)/shard_map/while/body/eval_jaxpr/conv_general_dilated | solution.py:34
  299.9 5.4 %select_add_fusion.2 = f32[24,8,9,768]{3,1,2,0:T(8,128)S(1)} fusion(f32[768]{0:T(1024)S(1)} %dynamic-slice_reduce_fusion.2, pred[8,9]{0,1:T(8,128)(4,1)S(1)} %get-tuple-element.146, bf16[3,3,192,768]{3,2,1,0:T(8,128)(2,1)S(1)} %copy-done.1, bf16[26,1,7,2,192]{4,2,3,0,1:T(8,128)(2,1)S(1)} %slice.80, bf16[26,1,8,9,192]{4,2,3,0,1:T(8,128)(2,1)S(1)} %copy.24), kind=kOutput, calls=%fused_computation.clone.1 | convolution fusion | flops 4591761408 | bytes 8824392 | tf_op jit(solution)/shard_map/while/body/eval_jaxpr/conv_general_dilated | solution.py:34
  330.2 5.4 %select_add_fusion.2 = f32[24,8,9,768]{3,1,2,0:T(8,128)S(1)} fusion(f32[768]{0:T(1024)S(1)} %dynamic-slice_reduce_fusion.2, pred[8,9]{0,1:T(8,128)(4,1)S(1)} %get-tuple-element.146, bf16[3,3,192,768]{3,2,1,0:T(8,128)(2,1)S(1)} %copy-done.1, bf16[26,1,7,2,192]{4,2,3,0,1:T(8,128)(2,1)S(1)} %slice.80, bf16[26,1,8,9,192]{4,2,3,0,1:T(8,128)(2,1)S(1)} %copy.24), kind=kOutput, calls=%fused_computation.clone.1 | convolution fusion | flops 4591761408 | bytes 8824392 | tf_op jit(solution)/shard_map/while/body/eval_jaxpr/conv_general_dilated | solution.py:34
  360.5 5.4 %select_add_fusion.2 = f32[24,8,9,768]{3,1,2,0:T(8,128)S(1)} fusion(f32[768]{0:T(1024)S(1)} %dynamic-slice_reduce_fusion.2, pred[8,9]{0,1:T(8,128)(4,1)S(1)} %get-tuple-element.146, bf16[3,3,192,768]{3,2,1,0:T(8,128)(2,1)S(1)} %copy-done.1, bf16[26,1,7,2,192]{4,2,3,0,1:T(8,128)(2,1)S(1)} %slice.80, bf16[26,1,8,9,192]{4,2,3,0,1:T(8,128)(2,1)S(1)} %copy.24), kind=kOutput, calls=%fused_computation.clone.1 | convolution fusion | flops 4591761408 | bytes 8824392 | tf_op jit(solution)/shard_map/while/body/eval_jaxpr/conv_general_dilated | solution.py:34
  390.8 5.4 %select_add_fusion.2 = f32[24,8,9,768]{3,1,2,0:T(8,128)S(1)} fusion(f32[768]{0:T(1024)S(1)} %dynamic-slice_reduce_fusion.2, pred[8,9]{0,1:T(8,128)(4,1)S(1)} %get-tuple-element.146, bf16[3,3,192,768]{3,2,1,0:T(8,128)(2,1)S(1)} %copy-done.1, bf16[26,1,7,2,192]{4,2,3,0,1:T(8,128)(2,1)S(1)} %slice.80, bf16[26,1,8,9,192]{4,2,3,0,1:T(8,128)(2,1)S(1)} %copy.24), kind=kOutput, calls=%fused_computation.clone.1 | convolution fusion | flops 4591761408 | bytes 8824392 | tf_op jit(solution)/shard_map/while/body/eval_jaxpr/conv_general_dilated | solution.py:34
  421.1 5.4 %select_add_fusion.2 = f32[24,8,9,768]{3,1,2,0:T(8,128)S(1)} fusion(f32[768]{0:T(1024)S(1)} %dynamic-slice_reduce_fusion.2, pred[8,9]{0,1:T(8,128)(4,1)S(1)} %get-tuple-element.146, bf16[3,3,192,768]{3,2,1,0:T(8,128)(2,1)S(1)} %copy-done.1, bf16[26,1,7,2,192]{4,2,3,0,1:T(8,128)(2,1)S(1)} %slice.80, bf16[26,1,8,9,192]{4,2,3,0,1:T(8,128)(2,1)S(1)} %copy.24), kind=kOutput, calls=%fused_computation.clone.1 | convolution fusion | flops 4591761408 | bytes 8824392 | tf_op jit(solution)/shard_map/while/body/eval_jaxpr/conv_general_dilated | solution.py:34
  451.4 5.4 %select_add_fusion.2 = f32[24,8,9,768]{3,1,2,0:T(8,128)S(1)} fusion(f32[768]{0:T(1024)S(1)} %dynamic-slice_reduce_fusion.2, pred[8,9]{0,1:T(8,128)(4,1)S(1)} %get-tuple-element.146, bf16[3,3,192,768]{3,2,1,0:T(8,128)(2,1)S(1)} %copy-done.1, bf16[26,1,7,2,192]{4,2,3,0,1:T(8,128)(2,1)S(1)} %slice.80, bf16[26,1,8,9,192]{4,2,3,0,1:T(8,128)(2,1)S(1)} %copy.24), kind=kOutput, calls=%fused_computation.clone.1 | convolution fusion | flops 4591761408 | bytes 8824392 | tf_op jit(solution)/shard_map/while/body/eval_jaxpr/conv_general_dilated | solution.py:34
  481.7 5.4 %select_add_fusion.2 = f32[24,8,9,768]{3,1,2,0:T(8,128)S(1)} fusion(f32[768]{0:T(1024)S(1)} %dynamic-slice_reduce_fusion.2, pred[8,9]{0,1:T(8,128)(4,1)S(1)} %get-tuple-element.146, bf16[3,3,192,768]{3,2,1,0:T(8,128)(2,1)S(1)} %copy-done.1, bf16[26,1,7,2,192]{4,2,3,0,1:T(8,128)(2,1)S(1)} %slice.80, bf16[26,1,8,9,192]{4,2,3,0,1:T(8,128)(2,1)S(1)} %copy.24), kind=kOutput, calls=%fused_computation.clone.1 | convolution fusion | flops 4591761408 | bytes 8824392 | tf_op jit(solution)/shard_map/while/body/eval_jaxpr/conv_general_dilated | solution.py:34
  (369 shorter events, 369.1 us)
Async XLA Ops:
  9.2 9.4 %collective-permute-start.2 = (bf16[1,26,1,192]{3,1,2,0:T(8,128)(2,1)S(1)}, bf16[1,26,1,192]{3,1,2,0:T(8,128)(2,1)S(1)}, u32[]{:S(2)}, u32[]{:S(2)}) collective-permute-start(bf16[1,26,1,192]{3,1,2,0:T(8,128)(2,1)S(1)} %get-tuple-element.114), channel_id=1, source_target_pairs={{2,0},{4,2},{6,4},{8,6},{10,8},{12,10},{14,12},{16,14},{18,16},{20... | collective-permute-start | bytes 29960 | tf_op jit(solution)/shard_map/while/body/eval_jaxpr/ppermute | solution.py:27
  15.9 8.7 %collective-permute-start.3 = (bf16[1,26,1,192]{3,1,2,0:T(8,128)(2,1)S(1)}, bf16[1,26,1,192]{3,1,2,0:T(8,128)(2,1)S(1)}, u32[]{:S(2)}, u32[]{:S(2)}) collective-permute-start(bf16[1,26,1,192]{3,1,2,0:T(8,128)(2,1)S(1)} %get-tuple-element.115), channel_id=1, source_target_pairs={{0,2},{2,4},{4,6},{6,8},{8,10},{10,12},{12,14},{14,16},{16,18},{18... | collective-permute-start | bytes 29960 | tf_op jit(solution)/shard_map/while/body/eval_jaxpr/ppermute | solution.py:26
  46.4 8.7 %collective-permute-start.3 = (bf16[1,26,1,192]{3,1,2,0:T(8,128)(2,1)S(1)}, bf16[1,26,1,192]{3,1,2,0:T(8,128)(2,1)S(1)}, u32[]{:S(2)}, u32[]{:S(2)}) collective-permute-start(bf16[1,26,1,192]{3,1,2,0:T(8,128)(2,1)S(1)} %get-tuple-element.115), channel_id=1, source_target_pairs={{0,2},{2,4},{4,6},{6,8},{8,10},{10,12},{12,14},{14,16},{16,18},{18... | collective-permute-start | bytes 29960 | tf_op jit(solution)/shard_map/while/body/eval_jaxpr/ppermute | solution.py:26
  74.8 6.1 %collective-permute-start.2 = (bf16[1,26,1,192]{3,1,2,0:T(8,128)(2,1)S(1)}, bf16[1,26,1,192]{3,1,2,0:T(8,128)(2,1)S(1)}, u32[]{:S(2)}, u32[]{:S(2)}) collective-permute-start(bf16[1,26,1,192]{3,1,2,0:T(8,128)(2,1)S(1)} %get-tuple-element.114), channel_id=1, source_target_pairs={{2,0},{4,2},{6,4},{8,6},{10,8},{12,10},{14,12},{16,14},{18,16},{20... | collective-permute-start | bytes 29960 | tf_op jit(solution)/shard_map/while/body/eval_jaxpr/ppermute | solution.py:27
  76.7 8.7 %collective-permute-start.3 = (bf16[1,26,1,192]{3,1,2,0:T(8,128)(2,1)S(1)}, bf16[1,26,1,192]{3,1,2,0:T(8,128)(2,1)S(1)}, u32[]{:S(2)}, u32[]{:S(2)}) collective-permute-start(bf16[1,26,1,192]{3,1,2,0:T(8,128)(2,1)S(1)} %get-tuple-element.115), channel_id=1, source_target_pairs={{0,2},{2,4},{4,6},{6,8},{8,10},{10,12},{12,14},{14,16},{16,18},{18... | collective-permute-start | bytes 29960 | tf_op jit(solution)/shard_map/while/body/eval_jaxpr/ppermute | solution.py:26
  105.1 6.1 %collective-permute-start.2 = (bf16[1,26,1,192]{3,1,2,0:T(8,128)(2,1)S(1)}, bf16[1,26,1,192]{3,1,2,0:T(8,128)(2,1)S(1)}, u32[]{:S(2)}, u32[]{:S(2)}) collective-permute-start(bf16[1,26,1,192]{3,1,2,0:T(8,128)(2,1)S(1)} %get-tuple-element.114), channel_id=1, source_target_pairs={{2,0},{4,2},{6,4},{8,6},{10,8},{12,10},{14,12},{16,14},{18,16},{20... | collective-permute-start | bytes 29960 | tf_op jit(solution)/shard_map/while/body/eval_jaxpr/ppermute | solution.py:27
  107.0 8.7 %collective-permute-start.3 = (bf16[1,26,1,192]{3,1,2,0:T(8,128)(2,1)S(1)}, bf16[1,26,1,192]{3,1,2,0:T(8,128)(2,1)S(1)}, u32[]{:S(2)}, u32[]{:S(2)}) collective-permute-start(bf16[1,26,1,192]{3,1,2,0:T(8,128)(2,1)S(1)} %get-tuple-element.115), channel_id=1, source_target_pairs={{0,2},{2,4},{4,6},{6,8},{8,10},{10,12},{12,14},{14,16},{16,18},{18... | collective-permute-start | bytes 29960 | tf_op jit(solution)/shard_map/while/body/eval_jaxpr/ppermute | solution.py:26
  137.3 8.7 %collective-permute-start.3 = (bf16[1,26,1,192]{3,1,2,0:T(8,128)(2,1)S(1)}, bf16[1,26,1,192]{3,1,2,0:T(8,128)(2,1)S(1)}, u32[]{:S(2)}, u32[]{:S(2)}) collective-permute-start(bf16[1,26,1,192]{3,1,2,0:T(8,128)(2,1)S(1)} %get-tuple-element.115), channel_id=1, source_target_pairs={{0,2},{2,4},{4,6},{6,8},{8,10},{10,12},{12,14},{14,16},{16,18},{18... | collective-permute-start | bytes 29960 | tf_op jit(solution)/shard_map/while/body/eval_jaxpr/ppermute | solution.py:26
  165.7 6.1 %collective-permute-start.2 = (bf16[1,26,1,192]{3,1,2,0:T(8,128)(2,1)S(1)}, bf16[1,26,1,192]{3,1,2,0:T(8,128)(2,1)S(1)}, u32[]{:S(2)}, u32[]{:S(2)}) collective-permute-start(bf16[1,26,1,192]{3,1,2,0:T(8,128)(2,1)S(1)} %get-tuple-element.114), channel_id=1, source_target_pairs={{2,0},{4,2},{6,4},{8,6},{10,8},{12,10},{14,12},{16,14},{18,16},{20... | collective-permute-start | bytes 29960 | tf_op jit(solution)/shard_map/while/body/eval_jaxpr/ppermute | solution.py:27
  167.6 8.7 %collective-permute-start.3 = (bf16[1,26,1,192]{3,1,2,0:T(8,128)(2,1)S(1)}, bf16[1,26,1,192]{3,1,2,0:T(8,128)(2,1)S(1)}, u32[]{:S(2)}, u32[]{:S(2)}) collective-permute-start(bf16[1,26,1,192]{3,1,2,0:T(8,128)(2,1)S(1)} %get-tuple-element.115), channel_id=1, source_target_pairs={{0,2},{2,4},{4,6},{6,8},{8,10},{10,12},{12,14},{14,16},{16,18},{18... | collective-permute-start | bytes 29960 | tf_op jit(solution)/shard_map/while/body/eval_jaxpr/ppermute | solution.py:26
  196.0 6.1 %collective-permute-start.2 = (bf16[1,26,1,192]{3,1,2,0:T(8,128)(2,1)S(1)}, bf16[1,26,1,192]{3,1,2,0:T(8,128)(2,1)S(1)}, u32[]{:S(2)}, u32[]{:S(2)}) collective-permute-start(bf16[1,26,1,192]{3,1,2,0:T(8,128)(2,1)S(1)} %get-tuple-element.114), channel_id=1, source_target_pairs={{2,0},{4,2},{6,4},{8,6},{10,8},{12,10},{14,12},{16,14},{18,16},{20... | collective-permute-start | bytes 29960 | tf_op jit(solution)/shard_map/while/body/eval_jaxpr/ppermute | solution.py:27
  197.9 8.7 %collective-permute-start.3 = (bf16[1,26,1,192]{3,1,2,0:T(8,128)(2,1)S(1)}, bf16[1,26,1,192]{3,1,2,0:T(8,128)(2,1)S(1)}, u32[]{:S(2)}, u32[]{:S(2)}) collective-permute-start(bf16[1,26,1,192]{3,1,2,0:T(8,128)(2,1)S(1)} %get-tuple-element.115), channel_id=1, source_target_pairs={{0,2},{2,4},{4,6},{6,8},{8,10},{10,12},{12,14},{14,16},{16,18},{18... | collective-permute-start | bytes 29960 | tf_op jit(solution)/shard_map/while/body/eval_jaxpr/ppermute | solution.py:26
  228.2 8.7 %collective-permute-start.3 = (bf16[1,26,1,192]{3,1,2,0:T(8,128)(2,1)S(1)}, bf16[1,26,1,192]{3,1,2,0:T(8,128)(2,1)S(1)}, u32[]{:S(2)}, u32[]{:S(2)}) collective-permute-start(bf16[1,26,1,192]{3,1,2,0:T(8,128)(2,1)S(1)} %get-tuple-element.115), channel_id=1, source_target_pairs={{0,2},{2,4},{4,6},{6,8},{8,10},{10,12},{12,14},{14,16},{16,18},{18... | collective-permute-start | bytes 29960 | tf_op jit(solution)/shard_map/while/body/eval_jaxpr/ppermute | solution.py:26
  256.6 6.1 %collective-permute-start.2 = (bf16[1,26,1,192]{3,1,2,0:T(8,128)(2,1)S(1)}, bf16[1,26,1,192]{3,1,2,0:T(8,128)(2,1)S(1)}, u32[]{:S(2)}, u32[]{:S(2)}) collective-permute-start(bf16[1,26,1,192]{3,1,2,0:T(8,128)(2,1)S(1)} %get-tuple-element.114), channel_id=1, source_target_pairs={{2,0},{4,2},{6,4},{8,6},{10,8},{12,10},{14,12},{16,14},{18,16},{20... | collective-permute-start | bytes 29960 | tf_op jit(solution)/shard_map/while/body/eval_jaxpr/ppermute | solution.py:27
  258.5 8.7 %collective-permute-start.3 = (bf16[1,26,1,192]{3,1,2,0:T(8,128)(2,1)S(1)}, bf16[1,26,1,192]{3,1,2,0:T(8,128)(2,1)S(1)}, u32[]{:S(2)}, u32[]{:S(2)}) collective-permute-start(bf16[1,26,1,192]{3,1,2,0:T(8,128)(2,1)S(1)} %get-tuple-element.115), channel_id=1, source_target_pairs={{0,2},{2,4},{4,6},{6,8},{8,10},{10,12},{12,14},{14,16},{16,18},{18... | collective-permute-start | bytes 29960 | tf_op jit(solution)/shard_map/while/body/eval_jaxpr/ppermute | solution.py:26
  286.9 6.1 %collective-permute-start.2 = (bf16[1,26,1,192]{3,1,2,0:T(8,128)(2,1)S(1)}, bf16[1,26,1,192]{3,1,2,0:T(8,128)(2,1)S(1)}, u32[]{:S(2)}, u32[]{:S(2)}) collective-permute-start(bf16[1,26,1,192]{3,1,2,0:T(8,128)(2,1)S(1)} %get-tuple-element.114), channel_id=1, source_target_pairs={{2,0},{4,2},{6,4},{8,6},{10,8},{12,10},{14,12},{16,14},{18,16},{20... | collective-permute-start | bytes 29960 | tf_op jit(solution)/shard_map/while/body/eval_jaxpr/ppermute | solution.py:27
  288.8 8.7 %collective-permute-start.3 = (bf16[1,26,1,192]{3,1,2,0:T(8,128)(2,1)S(1)}, bf16[1,26,1,192]{3,1,2,0:T(8,128)(2,1)S(1)}, u32[]{:S(2)}, u32[]{:S(2)}) collective-permute-start(bf16[1,26,1,192]{3,1,2,0:T(8,128)(2,1)S(1)} %get-tuple-element.115), channel_id=1, source_target_pairs={{0,2},{2,4},{4,6},{6,8},{8,10},{10,12},{12,14},{14,16},{16,18},{18... | collective-permute-start | bytes 29960 | tf_op jit(solution)/shard_map/while/body/eval_jaxpr/ppermute | solution.py:26
  319.1 8.7 %collective-permute-start.3 = (bf16[1,26,1,192]{3,1,2,0:T(8,128)(2,1)S(1)}, bf16[1,26,1,192]{3,1,2,0:T(8,128)(2,1)S(1)}, u32[]{:S(2)}, u32[]{:S(2)}) collective-permute-start(bf16[1,26,1,192]{3,1,2,0:T(8,128)(2,1)S(1)} %get-tuple-element.115), channel_id=1, source_target_pairs={{0,2},{2,4},{4,6},{6,8},{8,10},{10,12},{12,14},{14,16},{16,18},{18... | collective-permute-start | bytes 29960 | tf_op jit(solution)/shard_map/while/body/eval_jaxpr/ppermute | solution.py:26
  347.5 6.1 %collective-permute-start.2 = (bf16[1,26,1,192]{3,1,2,0:T(8,128)(2,1)S(1)}, bf16[1,26,1,192]{3,1,2,0:T(8,128)(2,1)S(1)}, u32[]{:S(2)}, u32[]{:S(2)}) collective-permute-start(bf16[1,26,1,192]{3,1,2,0:T(8,128)(2,1)S(1)} %get-tuple-element.114), channel_id=1, source_target_pairs={{2,0},{4,2},{6,4},{8,6},{10,8},{12,10},{14,12},{16,14},{18,16},{20... | collective-permute-start | bytes 29960 | tf_op jit(solution)/shard_map/while/body/eval_jaxpr/ppermute | solution.py:27
  349.4 8.7 %collective-permute-start.3 = (bf16[1,26,1,192]{3,1,2,0:T(8,128)(2,1)S(1)}, bf16[1,26,1,192]{3,1,2,0:T(8,128)(2,1)S(1)}, u32[]{:S(2)}, u32[]{:S(2)}) collective-permute-start(bf16[1,26,1,192]{3,1,2,0:T(8,128)(2,1)S(1)} %get-tuple-element.115), channel_id=1, source_target_pairs={{0,2},{2,4},{4,6},{6,8},{8,10},{10,12},{12,14},{14,16},{16,18},{18... | collective-permute-start | bytes 29960 | tf_op jit(solution)/shard_map/while/body/eval_jaxpr/ppermute | solution.py:26
  379.7 8.7 %collective-permute-start.3 = (bf16[1,26,1,192]{3,1,2,0:T(8,128)(2,1)S(1)}, bf16[1,26,1,192]{3,1,2,0:T(8,128)(2,1)S(1)}, u32[]{:S(2)}, u32[]{:S(2)}) collective-permute-start(bf16[1,26,1,192]{3,1,2,0:T(8,128)(2,1)S(1)} %get-tuple-element.115), channel_id=1, source_target_pairs={{0,2},{2,4},{4,6},{6,8},{8,10},{10,12},{12,14},{14,16},{16,18},{18... | collective-permute-start | bytes 29960 | tf_op jit(solution)/shard_map/while/body/eval_jaxpr/ppermute | solution.py:26
  410.0 8.7 %collective-permute-start.3 = (bf16[1,26,1,192]{3,1,2,0:T(8,128)(2,1)S(1)}, bf16[1,26,1,192]{3,1,2,0:T(8,128)(2,1)S(1)}, u32[]{:S(2)}, u32[]{:S(2)}) collective-permute-start(bf16[1,26,1,192]{3,1,2,0:T(8,128)(2,1)S(1)} %get-tuple-element.115), channel_id=1, source_target_pairs={{0,2},{2,4},{4,6},{6,8},{8,10},{10,12},{12,14},{14,16},{16,18},{18... | collective-permute-start | bytes 29960 | tf_op jit(solution)/shard_map/while/body/eval_jaxpr/ppermute | solution.py:26
  440.3 8.7 %collective-permute-start.3 = (bf16[1,26,1,192]{3,1,2,0:T(8,128)(2,1)S(1)}, bf16[1,26,1,192]{3,1,2,0:T(8,128)(2,1)S(1)}, u32[]{:S(2)}, u32[]{:S(2)}) collective-permute-start(bf16[1,26,1,192]{3,1,2,0:T(8,128)(2,1)S(1)} %get-tuple-element.115), channel_id=1, source_target_pairs={{0,2},{2,4},{4,6},{6,8},{8,10},{10,12},{12,14},{14,16},{16,18},{18... | collective-permute-start | bytes 29960 | tf_op jit(solution)/shard_map/while/body/eval_jaxpr/ppermute | solution.py:26
  470.6 8.7 %collective-permute-start.3 = (bf16[1,26,1,192]{3,1,2,0:T(8,128)(2,1)S(1)}, bf16[1,26,1,192]{3,1,2,0:T(8,128)(2,1)S(1)}, u32[]{:S(2)}, u32[]{:S(2)}) collective-permute-start(bf16[1,26,1,192]{3,1,2,0:T(8,128)(2,1)S(1)} %get-tuple-element.115), channel_id=1, source_target_pairs={{0,2},{2,4},{4,6},{6,8},{8,10},{10,12},{12,14},{14,16},{16,18},{18... | collective-permute-start | bytes 29960 | tf_op jit(solution)/shard_map/while/body/eval_jaxpr/ppermute | solution.py:26
  (58 other events, 201.6 us)
where the time goes:
time: 498 us; the launch traced here: 494 us
  starting transfers between devices  160 us (32%)
  waiting for transfers between devices  104 us (21%)
  local copies, waits for them, and re-layouts  90 us (18%)
  matrix products  86.7 us (17%)
  other arithmetic  51.1 us (10%)
    conv_general_dilated x16, matrix products, one_step(): lax.conv_general_dilated(padded, w_rec, (1, 1), 'VALID', dimension_number...  86.7 us
    ppermute x16, waiting for transfers between devices, with_halo(): from_left = lax.ppermute(tall_tile[:, :, -1:], 'cols', cols_right)  74.4 us
    ppermute x16, starting transfers between devices, with_halo(): from_left = lax.ppermute(tall_tile[:, :, -1:], 'cols', cols_right)  52.4 us
    ppermute x16, starting transfers between devices, with_halo(): from_below = lax.ppermute(tile[:, :1], 'rows', rows_up)  51.1 us
    ppermute x16, starting transfers between devices, with_halo(): from_right = lax.ppermute(tall_tile[:, :, :1], 'cols', cols_left)  35.5 us
    ppermute x16, waiting for transfers between devices, with_halo(): from_above = lax.ppermute(tile[:, -1:], 'rows', rows_down)  29.4 us
    div x16, other arithmetic, lstm_update(): jax.nn.sigmoid(forget_gate) * c_prev  26.2 us
    ppermute x16, starting transfers between devices, with_halo(): from_above = lax.ppermute(tile[:, -1:], 'rows', rows_down)  20.7 us
  transfers between devices with their start and end apart: 64, of which 32 were waited for; matrix products, arithmetic and copies ran while one was open for 2% of the time, Pallas kernels for 0%

commit v1 on v0

v1 whole, which is shorter than its diff:
```python
import functools

import jax
import jax.numpy as jnp
from jax import lax
from jax.experimental import pallas as pl
from jax.experimental.pallas import tpu as pltpu
from jax.sharding import PartitionSpec as P

MESH = pl.DeviceIdType.MESH
F32 = jnp.float32
BF16 = jnp.bfloat16

STEPS = 16
ROWS = 24
COLS = 64
CH = 192
LANES = 128
HALF = 64
EDGE = 8
INNER = 48
PITCH = 80
GROWS = ROWS + 3
GATES = 4 * CH
DEPTH = 14 * LANES
WIDTH = 5 * LANES
EXT = 2 * ROWS
STRIP = 32

I_ROWS = [range(6 * j, 6 * j + 6) for j in range(4)]
E_ROWS = [range(9), range(9, ROWS)]


def lanes(n, count=1):
    return slice(LANES * n, LANES * (n + count))


def sigmoid(x):
    return 0.5 * jnp.tanh(0.5 * x) + 0.5


def at_row(r):
    return r * PITCH + EDGE


def kernel(h_init, c_init, w_hbm, bias_ref, h_seq, c_last, w_ref, ws_ref, fa0, fb0, fa1, fb1, hb0, hb1, ca, cb, sb, el, er,
           out0, out1, cio, bp, to_right, to_left, from_left, from_right, diag_left, diag_right, seam,
           w_sems, in_sems, out_sems, col_send, left_recv, right_recv, dleft_recv, dright_recv, seam_send, seam_recv):
    col_count = lax.axis_size("cols")
    core = lax.axis_index("rows")
    col = lax.axis_index("cols")
    other = 1 - core
    has_left = col > 0
    has_right = col < col_count - 1

    def out_row(y):
        return jnp.where(core == 0, y, ROWS - 1 - y)

    in_copies = [pltpu.make_async_copy(src.at[0], dst, in_sems.at[n]) for n, (src, dst) in enumerate(((h_init, out0), (c_init, cio)))]
    for copy in in_copies:
        copy.start()
    w_copies = []
    for d in range(3):
        kd = jnp.where(core == 0, d, 2 - d)
        first = 4 * LANES * d
        pieces = [(first + LANES * dx, dx, 0, LANES) for dx in range(3)] + [(first + 3 * LANES + HALF * dx, dx, LANES, HALF) for dx in range(2)]
        for dst, dx, ch, size in pieces + [(12 * LANES + HALF * d, 2, LANES, HALF)]:
            w_copies.append(pltpu.make_async_copy(w_hbm.at[kd, dx, pl.ds(ch, size)], ws_ref.at[pl.ds(dst, size)], w_sems.at[len(w_copies)]))
    for copy in w_copies:
        copy.start()

    for ref in (fa0, fb0, fa1, fb1):
        ref[0:PITCH, :] = jnp.zeros((PITCH, LANES), F32)
        ref[(GROWS - 2) * PITCH:, :] = jnp.zeros((2 * PITCH, LANES), F32)
    for ref in (hb0, hb1):
        ref[0] = jnp.zeros((COLS, WIDTH), BF16)
    ws_ref[DEPTH - HALF:, :] = jnp.zeros((HALF, GATES), BF16)
    for ref in (el, er, from_left, from_right, diag_left, diag_right):
        ref[...] = jnp.zeros(ref.shape, F32)

    barrier = pltpu.get_barrier_semaphore()
    pl.semaphore_signal(barrier, inc=1, device_id={"rows": other}, device_id_type=MESH)
    for there, near in ((has_left, col - 1), (has_right, col + 1)):
        @pl.when(there)
        def _():
            pl.semaphore_signal(barrier, inc=1, device_id={"cols": near}, device_id_type=MESH)
            pl.semaphore_signal(barrier, inc=1, device_id={"cols": near, "rows": other}, device_id_type=MESH)

    low = lax.broadcasted_iota(jnp.int32, (1, LANES), 1) < HALF
    og_in = jnp.where(low, 0.5, 1.0).astype(F32)
    og_add = jnp.where(low, 0.5, 0.0).astype(F32)

    def sel(a, b):
        return jnp.where(low, a, b)

    def half_turn(x):
        return pltpu.roll(x, HALF, 1)

    def gate_blocks(t):
        return [t[0], half_turn(sel(t[2], t[1])), t[3], half_turn(sel(t[5], t[4])), sel(t[1], t[2]), sel(t[4], t[5])]

    for n, block in enumerate(gate_blocks([bias_ref[:, lanes(n)] for n in range(6)])):
        bp[:, lanes(n)] = block

    pl.semaphore_wait(barrier, 1 + 2 * has_left.astype(jnp.int32) + 2 * has_right.astype(jnp.int32))

    def side_copies(src, to, near, diag, slot, send, near_sem, diag_sem):
        return [
            pltpu.make_async_remote_copy(src, near.at[slot], col_send.at[send], near_sem.at[slot], device_id={"cols": to}, device_id_type=MESH),
            pltpu.make_async_remote_copy(src.at[:, pl.ds(ROWS - 8, 8)], diag.at[slot], col_send.at[send + 1], diag_sem.at[slot], device_id={"cols": to, "rows": other}, device_id_type=MESH),
        ]

    def columns(slot, start):
        def right():
            return side_copies(to_right, col + 1, from_left, diag_left, slot, 0, left_recv, dleft_recv)

        def left():
            return side_copies(to_left, col - 1, from_right, diag_right, slot, 2, right_recv, dright_recv)

        for there, copies, back in ((has_right, right, left), (has_left, left, right)):
            @pl.when(there)
            def _():
                for copy in copies():
                    copy.start() if start else copy.wait_send()
                if not start:
                    for copy in back():
                        copy.wait_recv()

    def seam_copies(slot):
        parts = [(ref, pl.ds(at_row(ROWS - k), COLS)) for k in range(2) for ref in (fa0, fb0)] + [(ref, pl.ds((ROWS - 1) * COLS, COLS)) for ref in (ca, cb)]
        return [
            pltpu.make_async_remote_copy(ref.at[rows], seam.at[slot, n], seam_send.at[n], seam_recv.at[slot, n], device_id={"rows": other}, device_id_type=MESH)
            for n, (ref, rows) in enumerate(parts)
        ]

    def column(ref, x, rows=ROWS):
        return ref[pl.ds(at_row(1) + x, rows, stride=PITCH), :]

    def build_messages():
        for out, a, b, lo, hi, x in ((to_right, 62, 63, 62, 63, 63), (to_left, 0, 1, 1, 0, 0)):
            out[0] = column(fa0, a)
            out[1] = column(fa0, b)
            out[2] = sel(column(fb0, lo), column(fb0, hi))
            out[3] = ca[pl.ds(x, ROWS, stride=COLS), :]
            out[4] = cb[pl.ds(x, ROWS, stride=COLS), :]

    def insert_halos(slot):
        for k in range(2):
            for n, ref in enumerate((fa0, fb0)):
                ref[at_row(ROWS + 1 + k):at_row(ROWS + 1 + k) + COLS, :] = seam[slot, 2 * k + n]
        for n, ref in enumerate((ca, cb)):
            ref[ROWS * COLS:, :] = seam[slot, 4 + n]
        for ext, box, corner, beside, own in ((el, from_left, diag_left, -1, 0), (er, from_right, diag_right, COLS, COLS - 1)):
            parts = [(slice(8, 8 + ROWS), [box[slot, n] for n in range(5)], column(fa0, own), column(fb0, own))]
            for k in range(2):
                cell = at_row(ROWS + 1 + k) + own
                parts.append((slice(8 + ROWS + k, 9 + ROWS + k), [corner[slot, n, 7 - k:8 - k] for n in range(5)], fa0[cell:cell + 1, :], fb0[cell:cell + 1, :]))
            for k, (rows, (a0, a1, p, c_a, c_b), own_a, own_b) in enumerate(parts):
                if beside < 0:
                    tiles = (a0, a1, own_a, p, own_b, c_a, c_b)
                    near = a1
                else:
                    tiles = (own_a, a0, a1, sel(own_b, p), sel(p, half_turn(p)), c_a, c_b)
                    near = a0
                for n, tile in enumerate(tiles):
                    ext[n, rows, :] = tile
                far = sel(half_turn(p), p)
                if k == 0:
                    cells = pl.ds(at_row(1) + beside, ROWS, stride=PITCH)
                else:
                    cells = pl.ds(at_row(ROWS + k) + beside, 1)
                fa0[cells, :] = near
                fb0[cells, :] = far

        def both(n, e):
            return jnp.concatenate([ext[n, 7 + e:7 + e + STRIP, :] for ext in (el, er)], axis=0)

        for e in range(3):
            for n in range(4):
                sb[:, lanes(4 * e + n)] = both(n, e).astype(BF16)
        sb[:, lanes(12)] = sel(both(4, 0), both(4, 1)).astype(BF16)
        sb[:, lanes(13)] = both(4, 2).astype(BF16)

    def put_operands(hb, r, cells, a, b):
        for n in range(3):
            hb[r, cells, lanes(n)] = a[n].astype(BF16)
        hb[r, cells, lanes(3)] = sel(b[0], b[1]).astype(BF16)
        hb[r, cells, lanes(4)] = b[2].astype(BF16)

    def assemble_inner(fa, fb, hb, r):
        at = at_row(r) + EDGE
        a, b = ([ref[at + s:at + s + INNER, :] for s in (-1, 0, 1)] for ref in (fa, fb))
        put_operands(hb, r, slice(0, INNER), a, b)

    def assemble_edge(fa, fb, hb, r):
        at = at_row(r)
        a, b = ([jnp.concatenate([ref[x + s:x + s + EDGE, :] for x in (at, at + COLS - EDGE)], axis=0) for s in (-1, 0, 1)] for ref in (fa, fb))
        put_operands(hb, r, slice(INNER, COLS), a, b)

    def write_out(fa, fb, out, y):
        at = at_row(y + 1)
        row = out_row(y)
        out[row, :, 0:LANES] = fa[at:at + COLS, :].astype(BF16)
        out[row, :, LANES:CH] = fb[at:at + COLS, 0:HALF].astype(BF16)

    def gates(z, bias, c_a, c_b):
        z = [z[:, lanes(n)] + bias[:, lanes(n)] for n in range(6)]
        ca_new = sigmoid(z[1]) * c_a + sigmoid(z[0]) * jnp.tanh(z[3])
        h_a = sigmoid(z[2]) * jnp.tanh(ca_new)
        out_cand = jnp.tanh(z[5] * og_in) * og_in + og_add
        turned = half_turn(out_cand)
        terms = sigmoid(z[4]) * sel(turned, c_b)
        cb_new = terms + half_turn(terms)
        h_b = sel(out_cand, turned) * jnp.tanh(cb_new)
        return h_a, h_b, ca_new, cb_new

    def unit_rows(unit):
        kind, y, count = unit
        return {"I": INNER, "E": 2 * EDGE * count, "S": 2 * STRIP}[kind]

    def unit_lhs(hb, unit):
        kind, y, count = unit
        if kind == "S":
            return sb[...]

        def block(r, part):
            if kind == "I":
                return hb[r, 0:INNER, part]
            return hb[r:r + count, INNER:COLS, part].reshape(unit_rows(unit), part.stop - part.start)

        near = [block(y + e, lanes(0, 4)) for e in range(3)]
        far = [block(y + e, lanes(4)) for e in range(3)]
        return jnp.concatenate(near + [sel(far[0], far[1]), far[2]], axis=1)

    def unit_gates(unit, z, bias, fa, fb):
        kind, y, count = unit
        if kind == "S":
            c_a, c_b = (jnp.concatenate([ext[n, 8:8 + STRIP, :] for ext in (el, er)], axis=0) for n in (5, 6))
            h_a, h_b, _, _ = gates(z, bias, c_a, c_b)
            for beside, first, there in ((-1, 0, has_left), (COLS, STRIP, has_right)):
                for ref, h in ((fa, h_a), (fb, h_b)):
                    h = jnp.where(there, h[first:first + STRIP], 0.0)
                    ref[pl.ds(at_row(1) + beside, ROWS, stride=PITCH), :] = h[0:ROWS]
                    ref[pl.ds(at_row(ROWS + 1) + beside, 1), :] = h[ROWS:ROWS + 1]
            return
        if kind == "I":
            spans = [(y, EDGE, INNER)]
        else:
            spans = [(y + n, x, EDGE) for n in range(count) for x in (0, COLS - EDGE)]
        cells = [slice(r * COLS + x, r * COLS + x + size) for r, x, size in spans]
        c_a, c_b = (jnp.concatenate([ref[part, :] for part in cells], axis=0) for ref in (ca, cb))
        h_a, h_b, ca_new, cb_new = gates(z, bias, c_a, c_b)
        done = 0
        for (r, x, size), part in zip(spans, cells):
            to = slice(at_row(r + 1) + x, at_row(r + 1) + x + size)
            for ref, where, value in ((fa, to, h_a), (fb, to, h_b), (ca, part, ca_new), (cb, part, cb_new)):
                ref[where, :] = value[done:done + size]
            done += size

    i_units = [[("I", y, 1) for y in rows] for rows in I_ROWS]
    e_units = [[("E", y, 3) for y in rows[::3]] for rows in E_ROWS]
    old, new = (fa0, fb0), (fa1, fb1)
    results = [None, None]

    def piece(parity, hb, units, tasks):
        lhs = jnp.concatenate([unit_lhs(hb, unit) for unit in units], axis=0)
        results[parity] = jnp.dot(lhs, w_ref[...], preferred_element_type=F32)
        for task in tasks:
            task()

    def gate_tasks(parity, units, bias, state):
        z = results[parity]
        tasks, first = [], 0
        for unit in units:
            size = unit_rows(unit)
            tasks.append(functools.partial(unit_gates, unit, z[first:first + size], bias, *state))
            first += size
        return tasks

    def inner_tasks(state, hb, rows):
        return [functools.partial(assemble_inner, *state, hb, r) for r in rows]

    def edge_tasks(state, hb, rows):
        return [functools.partial(assemble_edge, *state, hb, r) for r in rows]

    def out_tasks(state, out, rows):
        return [functools.partial(write_out, *state, out, y) for y in rows]

    def out_copy(out, t, n):
        return pltpu.make_async_copy(out, h_seq.at[t, 0], out_sems.at[n])

    for copy in in_copies:
        copy.wait()

    def load_row(y, _):
        row = out_row(y)
        h = out0[row].astype(F32)
        c = cio[row]
        to = pl.ds(pl.multiple_of(at_row(y + 1), 8), COLS)
        cells = pl.ds(pl.multiple_of(y * COLS, COLS), COLS)
        for a, b, where, value in ((fa0, fb0, to, h), (ca, cb, cells, c)):
            a[where, :] = value[:, 0:LANES]
            b[where, :] = jnp.concatenate([value[:, LANES:CH]] * 2, axis=1)
        return 0

    lax.fori_loop(0, ROWS, load_row, 0)
    build_messages()

    def load_weights(n, _):
        rows = pl.ds(pl.multiple_of(n * HALF, HALF), HALF)
        blocks = gate_blocks([ws_ref[rows, lanes(i)].astype(F32) for i in range(6)])
        for i, block in enumerate(blocks):
            w_ref[rows, lanes(i)] = block.astype(BF16)
        return 0

    for copy in w_copies:
        copy.wait()
    columns(0, True)
    for copy in seam_copies(0):
        copy.start()
    lax.fori_loop(0, DEPTH // HALF, load_weights, 0)
    for r in range(1, ROWS + 1):
        assemble_inner(*old, hb0, r)

    def two_steps(s, _):
        slot = lax.rem(s, 2)
        more = s < STEPS // 2 - 1
        bias_a = bp[pl.ds(2 * s, 1), :]
        bias_b = bp[pl.ds(2 * s + 1, 1), :]

        piece(0, hb0, i_units[0], [])
        piece(1, hb0, i_units[1], gate_tasks(0, i_units[0], bias_a, new))
        piece(0, hb0, i_units[2], gate_tasks(1, i_units[1], bias_a, new))
        for copy in seam_copies(slot):
            copy.wait()
        columns(slot, False)

        @pl.when(s > 0)
        def _():
            for n, out in enumerate((out0, out1)):
                out_copy(out, 2 * s - 2 + n, n).wait()

        insert_halos(slot)
        for r in range(1, GROWS):
            assemble_edge(*old, hb0, r)
        for r in range(ROWS + 1, GROWS):
            assemble_inner(*old, hb0, r)
        extra = e_units[0] + [("S", 0, 0), ("E", ROWS, 1)]
        last = i_units[3] + [("I", ROWS, 1)]
        piece(1, hb0, e_units[1], gate_tasks(0, i_units[2], bias_a, new))
        piece(0, hb0, extra, gate_tasks(1, e_units[1], bias_a, new))
        piece(1, hb0, last, gate_tasks(0, extra, bias_a, new) + edge_tasks(new, hb1, range(1, 11)))

        piece(0, hb1, e_units[0], gate_tasks(1, last, bias_a, new) + edge_tasks(new, hb1, range(11, ROWS + 2)))
        piece(1, hb1, e_units[1], gate_tasks(0, e_units[0], bias_b, old) + inner_tasks(new, hb1, range(18, ROWS + 2)))
        piece(0, hb1, i_units[3], gate_tasks(1, e_units[1], bias_b, old) + inner_tasks(new, hb1, range(1, 8)))

        @pl.when(more)
        def _():
            build_messages()
            columns(1 - slot, True)

        piece(1, hb1, i_units[0], gate_tasks(0, i_units[3], bias_b, old) + inner_tasks(new, hb1, range(8, 18)) + inner_tasks(old, hb0, range(19, ROWS + 1)))

        @pl.when(more)
        def _():
            for copy in seam_copies(1 - slot):
                copy.start()

        piece(0, hb1, i_units[1], gate_tasks(1, i_units[0], bias_b, old) + inner_tasks(old, hb0, range(1, 7)) + out_tasks(new, out0, range(ROWS)))
        tail = range(12, 18)
        rest = [y for y in range(ROWS) if y not in tail]
        piece(1, hb1, i_units[2], gate_tasks(0, i_units[1], bias_b, old) + inner_tasks(old, hb0, range(7, 13)) + out_tasks(old, out1, rest))
        for task in gate_tasks(1, i_units[2], bias_b, old) + inner_tasks(old, hb0, range(13, 19)) + out_tasks(old, out1, tail):
            task()
        for n, out in enumerate((out0, out1)):
            out_copy(out, 2 * s + n, n).start()
        return 0

    lax.fori_loop(0, STEPS // 2, two_steps, 0)

    def store_row(y, _):
        cells = pl.ds(pl.multiple_of(y * COLS, COLS), COLS)
        row = out_row(y)
        cio[row, :, 0:LANES] = ca[cells, :]
        cio[row, :, LANES:CH] = cb[cells, 0:HALF]
        return 0

    lax.fori_loop(0, ROWS, store_row, 0)
    c_copy = pltpu.make_async_copy(cio, c_last.at[0], in_sems.at[1])
    c_copy.start()
    for n, out in enumerate((out0, out1)):
        out_copy(out, STEPS - 2 + n, n).wait()
    c_copy.wait()


def solution(mesh):
    def device_fn(h_init, c_init, w_rec, gate_bias):
        hbm = pl.BlockSpec(memory_space=pltpu.HBM)
        vmem = pltpu.VMEM
        dma = pltpu.SemaphoreType.DMA
        tile = (ROWS, COLS, CH)
        edge = (5, ROWS, LANES)
        return pl.pallas_call(
            kernel,
            out_shape=(
                jax.ShapeDtypeStruct((STEPS, 1, *tile), BF16),
                jax.ShapeDtypeStruct((1, *tile), F32),
            ),
            in_specs=[hbm, hbm, hbm, pl.BlockSpec(memory_space=pltpu.VMEM)],
            out_specs=(hbm, hbm),
            scratch_shapes=[
                *[vmem((DEPTH, GATES), BF16)] * 2,
                *[vmem((GROWS * PITCH, LANES), F32)] * 4,
                *[vmem((GROWS, COLS, WIDTH), BF16)] * 2,
                *[vmem(((ROWS + 1) * COLS, LANES), F32)] * 2,
                vmem((2 * STRIP, DEPTH), BF16),
                *[vmem((7, EXT, LANES), F32)] * 2,
                *[vmem(tile, BF16)] * 2,
                vmem(tile, F32),
                vmem((STEPS, GATES), F32),
                *[vmem(edge, F32)] * 2,
                *[vmem((2, *edge), F32)] * 2,
                *[vmem((2, 5, 8, LANES), F32)] * 2,
                vmem((2, 6, COLS, LANES), F32),
                dma((18,)),
                dma((2,)),
                dma((2,)),
                dma((4,)),
                *[dma((2,))] * 4,
                dma((6,)),
                dma((2, 6)),
            ],
            compiler_params=pltpu.CompilerParams(collective_id=0, has_side_effects=True, vmem_limit_bytes=60 * 1024 * 1024),
        )(h_init, c_init, w_rec, gate_bias)

    state_spec = P("dp", "rows", "cols", None)
    return jax.shard_map(device_fn, mesh=mesh, in_specs=(state_spec, state_spec, P(), P()), out_specs=(P(None, "dp", "rows", "cols", None), state_spec), check_vma=False)
```

time: 498 us -> 114 us (0.23)
  starting transfers between devices: 160 us -> 0 us
  waiting for transfers between devices: 104 us -> 0 us
  Pallas kernels: 0 us -> 101 us
  matrix products: 86.7 us -> 0 us
  local copies, waits for them, and re-layouts: 90 us -> 12 us
  other arithmetic: 51.1 us -> 0 us
    ppermute x64 -> x0, starting transfers between devices: 160 us -> none  [the longest x16 52.4 us: with_halo(): from_left = lax.ppermute(tall_tile[:, :, -1:], 'cols', cols_right)]
    ppermute x64 -> x0, waiting for transfers between devices: 104 us -> none  [the longest x16 74.4 us: with_halo(): from_left = lax.ppermute(tall_tile[:, :, -1:], 'cols', cols_right)]
    pallas_call x0 -> x1, Pallas kernels: none -> 101 us  [device_fn(): pl.pallas_call(kernel, out_shape=(jax.ShapeDtypeStruct((STEPS, 1, *tile),...]
    conv_general_dilated x16 -> x0, matrix products: 86.7 us -> none  [one_step(): lax.conv_general_dilated(padded, w_rec, (1, 1), 'VALID', dimension_number...]
    div x16 -> x0, other arithmetic: 26.2 us -> none  [lstm_update(): jax.nn.sigmoid(forget_gate) * c_prev]
    div x32 -> x0, local copies, waits for them, and re-layouts: 18.3 us -> none  [lstm_update(): jax.nn.sigmoid(forget_gate) * c_prev]
    dynamic_update_slice x16 -> x0, local copies, waits for them, and re-layouts: 17 us -> none  [device_fn(): final_state, h_seq = lax.scan(one_step, (h_init, c_init), gate_bias)]
    while x34 -> x0, local copies, waits for them, and re-layouts: 16.5 us -> none
  transfers between devices with their start and end apart: 64 -> 0, of which waited for: 32 -> 0; matrix products, arithmetic and copies ran while one was open for 2% -> 0% of each run, Pallas kernels for 0% -> 0%
where the time goes in v1:
time: 114 us
  Pallas kernels  101 us (89%)
  local copies, waits for them, and re-layouts  12 us (11%)
    pallas_call x1, Pallas kernels, device_fn(): pl.pallas_call(kernel, out_shape=(jax.ShapeDtypeStruct((STEPS, 1, *tile),...  101 us
    unnamed x4, local copies, waits for them, and re-layouts  12 us

profile of v1, /device:TPU:97, one launch (start us, length us, event | category | flops | bytes accessed | tf_op | source)
XLA Modules:
  0.0 113.7 jit_solution(9519566052832076802)
XLA Ops:
  0.6 101.1 %shard_map.59 = (bf16[16,1,24,64,192]{4,3,2,1,0:T(8,128)(2,1)}, f32[1,24,64,192]{3,2,1,0:T(8,128)}) custom-call(bf16[1,24,64,192]{3,2,1,0:T(8,128)(2,1)} %h_init.1, f32[1,24,64,192]{3,2,1,0:T(8,128)} %c_init.1, bf16[3,3,192,768]{3,2,1,0:T(8,128)(2,1)} %w_hbm.1, f32[16,768]{1,0:T(8,128)} %bias_ref.1), custom_call_target="tpu_custom_call" | custom-call | tf_op jit(solution)/shard_map/pallas_call | solution.py:404
  101.7 0.0 copy-start
  101.7 10.9 %copy.8 = bf16[16,1,24,64,192]{4,3,2,1,0:T(8,128)(2,1)} copy(bf16[16,1,24,64,192]{4,3,2,1,0:T(8,128)(2,1)} %get-tuple-element.4) | data formatting | bytes 18874368
  112.6 0.0 copy-done
  112.6 1.1 %copy.9 = f32[1,24,64,192]{3,2,1,0:T(8,128)} copy(f32[1,24,64,192]{3,2,1,0:T(8,128)S(1)} %copy-done) | data formatting | bytes 2359296
Async XLA Ops:
  101.7 10.9 %copy-start = (f32[1,24,64,192]{3,2,1,0:T(8,128)S(1)}, f32[1,24,64,192]{3,2,1,0:T(8,128)}, u32[]{:S(2)}) copy-start(f32[1,24,64,192]{3,2,1,0:T(8,128)} %get-tuple-element.5) | copy-start | bytes 3538948

commit v2 on v1

--- a/solution.py
+++ b/solution.py
@@ -28,6 +28,8 @@
 STRIP = 32
 
 I_ROWS = [range(6 * j, 6 * j + 6) for j in range(4)]
+EARLY_ROWS = [range(6), range(6, 12), range(12, 17), range(17, 22)]
+LATE_ROWS = range(22, ROWS + 1)
 E_ROWS = [range(9), range(9, ROWS)]
 
 
@@ -44,7 +46,7 @@
 
 
 def kernel(h_init, c_init, w_hbm, bias_ref, h_seq, c_last, w_ref, ws_ref, fa0, fb0, fa1, fb1, hb0, hb1, ca, cb, sb, el, er,
-           out0, out1, cio, bp, to_right, to_left, from_left, from_right, diag_left, diag_right, seam,
+           out0, out1, cio, bp, zs, to_right, to_left, from_left, from_right, diag_left, diag_right, seam,
            w_sems, in_sems, out_sems, col_send, left_recv, right_recv, dleft_recv, dright_recv, seam_send, seam_recv):
     col_count = lax.axis_size("cols")
     core = lax.axis_index("rows")
@@ -172,6 +174,7 @@
                 fa0[cells, :] = near
                 fb0[cells, :] = far
 
+    def build_strips():
         def both(n, e):
             return jnp.concatenate([ext[n, 7 + e:7 + e + STRIP, :] for ext in (el, er)], axis=0)
 
@@ -232,7 +235,8 @@
         far = [block(y + e, lanes(4)) for e in range(3)]
         return jnp.concatenate(near + [sel(far[0], far[1]), far[2]], axis=1)
 
-    def unit_gates(unit, z, bias, fa, fb):
+    def unit_gates(unit, z, part, bias, fa, fb):
+        z = z[part, :]
         kind, y, count = unit
         if kind == "S":
             c_a, c_b = (jnp.concatenate([ext[n, 8:8 + STRIP, :] for ext in (el, er)], axis=0) for n in (5, 6))
@@ -257,23 +261,28 @@
                 ref[where, :] = value[done:done + size]
             done += size
 
-    i_units = [[("I", y, 1) for y in rows] for rows in I_ROWS]
+    def i_units(rows):
+        return [("I", y, 1) for y in rows]
+
     e_units = [[("E", y, 3) for y in rows[::3]] for rows in E_ROWS]
     old, new = (fa0, fb0), (fa1, fb1)
     results = [None, None]
 
     def piece(parity, hb, units, tasks):
         lhs = jnp.concatenate([unit_lhs(hb, unit) for unit in units], axis=0)
-        results[parity] = jnp.dot(lhs, w_ref[...], preferred_element_type=F32)
+        half = sum(unit_rows(unit) for unit in units[:(len(units) + 1) // 2])
+        wide = [jnp.dot(lhs, w_ref[:, lanes(2 * n, 2)], preferred_element_type=F32) for n in range(2)]
+        halves = [jnp.dot(part, w_ref[:, lanes(4, 2)], preferred_element_type=F32) for part in (lhs[:half], lhs[half:])]
+        results[parity] = jnp.concatenate(wide + [jnp.concatenate(halves, axis=0)], axis=1)
         for task in tasks:
             task()
 
     def gate_tasks(parity, units, bias, state):
-        z = results[parity]
+        z = zs if parity is None else results[parity]
         tasks, first = [], 0
         for unit in units:
             size = unit_rows(unit)
-            tasks.append(functools.partial(unit_gates, unit, z[first:first + size], bias, *state))
+            tasks.append(functools.partial(unit_gates, unit, z, slice(first, first + size), bias, *state))
             first += size
         return tasks
 
@@ -322,62 +331,80 @@
     for r in range(1, ROWS + 1):
         assemble_inner(*old, hb0, r)
 
-    def two_steps(s, _):
-        slot = lax.rem(s, 2)
-        more = s < STEPS // 2 - 1
-        bias_a = bp[pl.ds(2 * s, 1), :]
-        bias_b = bp[pl.ds(2 * s + 1, 1), :]
-
-        piece(0, hb0, i_units[0], [])
-        piece(1, hb0, i_units[1], gate_tasks(0, i_units[0], bias_a, new))
-        piece(0, hb0, i_units[2], gate_tasks(1, i_units[1], bias_a, new))
+    def bias_of(t):
+        return bp[pl.ds(t, 1), :]
+
+    def early(t, tasks):
+        units = [i_units(rows) for rows in EARLY_ROWS]
+        bias = bias_of(t)
+        for n in range(4):
+            more = gate_tasks(1 - n % 2, units[n - 1], bias, new) if n else []
+            piece(n % 2, hb0, units[n], more + tasks[n])
+        zs[...] = results[1]
+
+    def halos(slot):
         for copy in seam_copies(slot):
             copy.wait()
         columns(slot, False)
-
-        @pl.when(s > 0)
-        def _():
+        insert_halos(slot)
+
+    def rest(s, slot, last):
+        bias_a, bias_b = bias_of(2 * s), bias_of(2 * s + 1)
+        for r in range(1, 11):
+            assemble_edge(*old, hb0, r)
+
+        far = e_units[1] + [("S", 0, 0), ("E", ROWS, 1)]
+        late = i_units(LATE_ROWS)
+        piece(0, hb0, e_units[0], [build_strips] + edge_tasks(old, hb0, range(11, GROWS)) + gate_tasks(None, i_units(EARLY_ROWS[3]), bias_a, new))
+        piece(1, hb0, far, inner_tasks(old, hb0, range(ROWS + 1, GROWS)) + gate_tasks(0, e_units[0], bias_a, new))
+        piece(0, hb0, late, gate_tasks(1, far, bias_a, new) + edge_tasks(new, hb1, range(1, 11)))
+
+        rows = [i_units(part) for part in I_ROWS]
+        piece(1, hb1, e_units[0], gate_tasks(0, late, bias_a, new) + edge_tasks(new, hb1, range(11, ROWS + 2)))
+        piece(0, hb1, e_units[1], gate_tasks(1, e_units[0], bias_b, old) + inner_tasks(new, hb1, range(18, ROWS + 2)))
+        piece(1, hb1, rows[3], gate_tasks(0, e_units[1], bias_b, old) + inner_tasks(new, hb1, range(1, 8)))
+        piece(0, hb1, rows[0], gate_tasks(1, rows[3], bias_b, old) + inner_tasks(new, hb1, range(8, 18)))
+        if not last:
+            build_messages()
+            columns(1 - slot, True)
+            for copy in seam_copies(1 - slot):
+                copy.start()
+
+            @pl.when(s > 0)
+            def _():
+                for n, out in enumerate((out0, out1)):
+                    out_copy(out, 2 * s - 2 + n, n).wait()
+        else:
             for n, out in enumerate((out0, out1)):
                 out_copy(out, 2 * s - 2 + n, n).wait()
 
-        insert_halos(slot)
-        for r in range(1, GROWS):
-            assemble_edge(*old, hb0, r)
-        for r in range(ROWS + 1, GROWS):
-            assemble_inner(*old, hb0, r)
-        extra = e_units[0] + [("S", 0, 0), ("E", ROWS, 1)]
-        last = i_units[3] + [("I", ROWS, 1)]
-        piece(1, hb0, e_units[1], gate_tasks(0, i_units[2], bias_a, new))
-        piece(0, hb0, extra, gate_tasks(1, e_units[1], bias_a, new))
-        piece(1, hb0, last, gate_tasks(0, extra, bias_a, new) + edge_tasks(new, hb1, range(1, 11)))
-
-        piece(0, hb1, e_units[0], gate_tasks(1, last, bias_a, new) + edge_tasks(new, hb1, range(11, ROWS + 2)))
-        piece(1, hb1, e_units[1], gate_tasks(0, e_units[0], bias_b, old) + inner_tasks(new, hb1, range(18, ROWS + 2)))
-        piece(0, hb1, i_units[3], gate_tasks(1, e_units[1], bias_b, old) + inner_tasks(new, hb1, range(1, 8)))
-
-        @pl.when(more)
-        def _():
-            build_messages()
-            columns(1 - slot, True)
-
-        piece(1, hb1, i_units[0], gate_tasks(0, i_units[3], bias_b, old) + inner_tasks(new, hb1, range(8, 18)) + inner_tasks(old, hb0, range(19, ROWS + 1)))
-
-        @pl.when(more)
-        def _():
-            for copy in seam_copies(1 - slot):
-                copy.start()
-
-        piece(0, hb1, i_units[1], gate_tasks(1, i_units[0], bias_b, old) + inner_tasks(old, hb0, range(1, 7)) + out_tasks(new, out0, range(ROWS)))
-        tail = range(12, 18)
-        rest = [y for y in range(ROWS) if y not in tail]
-        piece(1, hb1, i_units[2], gate_tasks(0, i_units[1], bias_b, old) + inner_tasks(old, hb0, range(7, 13)) + out_tasks(old, out1, rest))
-        for task in gate_tasks(1, i_units[2], bias_b, old) + inner_tasks(old, hb0, range(13, 19)) + out_tasks(old, out1, tail):
-            task()
+        def next_operands(first, count):
+            return [] if last else inner_tasks(old, hb0, range(first, first + count))
+
+        piece(1, hb1, rows[1], gate_tasks(0, rows[0], bias_b, old) + next_operands(19, 6) + next_operands(1, 6) + out_tasks(new, out0, range(ROWS)))
+        piece(0, hb1, rows[2], gate_tasks(1, rows[1], bias_b, old) + next_operands(7, 6) + out_tasks(old, out1, I_ROWS[0]) + out_tasks(old, out1, I_ROWS[3]))
+        tail = gate_tasks(0, rows[2], bias_b, old) + next_operands(13, 6)
+        done = out_tasks(old, out1, I_ROWS[1]) + out_tasks(old, out1, I_ROWS[2])
+        if last:
+            for task in tail + done:
+                task()
+        else:
+            early(2 * s + 2, [tail, done[:6], done[6:], []])
         for n, out in enumerate((out0, out1)):
             out_copy(out, 2 * s + n, n).start()
+
+    early(0, [[], [], [], []])
+
+    def two_steps(s, _):
+        slot = lax.rem(s, 2)
+        halos(slot)
+        rest(s, slot, False)
         return 0
 
-    lax.fori_loop(0, STEPS // 2, two_steps, 0)
+    last_pair = STEPS // 2 - 1
+    lax.fori_loop(0, last_pair, two_steps, 0)
+    halos(last_pair % 2)
+    rest(last_pair, last_pair % 2, True)
 
     def store_row(y, _):
         cells = pl.ds(pl.multiple_of(y * COLS, COLS), COLS)
@@ -419,6 +446,7 @@
                 *[vmem(tile, BF16)] * 2,
                 vmem(tile, F32),
                 vmem((STEPS, GATES), F32),
+                vmem((len(EARLY_ROWS[3]) * INNER, GATES), F32),
                 *[vmem(edge, F32)] * 2,
                 *[vmem((2, *edge), F32)] * 2,
                 *[vmem((2, 5, 8, LANES), F32)] * 2,

time: 114 us -> 116 us (1.018)
  Pallas kernels: 101 us -> 103 us
    pallas_call x1, Pallas kernels: 101 us -> 103 us  [device_fn(): pl.pallas_call(kernel, out_shape=(jax.ShapeDtypeStruct((STEPS, 1, *tile),...]
where the time goes in v2:
time: 116 us
  Pallas kernels  103 us (89%)
  local copies, waits for them, and re-layouts  12 us (10%)
    pallas_call x1, Pallas kernels, device_fn(): pl.pallas_call(kernel, out_shape=(jax.ShapeDtypeStruct((STEPS, 1, *tile),...  103 us
    unnamed x4, local copies, waits for them, and re-layouts  12 us

profile of v2, /device:TPU:97, one launch (start us, length us, event | category | flops | bytes accessed | tf_op | source)
XLA Modules:
  0.0 115.7 jit_solution(2402933841083036274)
XLA Ops:
  0.6 103.1 %shard_map.59 = (bf16[16,1,24,64,192]{4,3,2,1,0:T(8,128)(2,1)}, f32[1,24,64,192]{3,2,1,0:T(8,128)}) custom-call(bf16[1,24,64,192]{3,2,1,0:T(8,128)(2,1)} %h_init.1, f32[1,24,64,192]{3,2,1,0:T(8,128)} %c_init.1, bf16[3,3,192,768]{3,2,1,0:T(8,128)(2,1)} %w_hbm.1, f32[16,768]{1,0:T(8,128)} %bias_ref.1), custom_call_target="tpu_custom_call" | custom-call | tf_op jit(solution)/shard_map/pallas_call | solution.py:431
  103.7 0.0 copy-start
  103.7 10.9 %copy.8 = bf16[16,1,24,64,192]{4,3,2,1,0:T(8,128)(2,1)} copy(bf16[16,1,24,64,192]{4,3,2,1,0:T(8,128)(2,1)} %get-tuple-element.4) | data formatting | bytes 18874368
  114.6 0.0 copy-done
  114.6 1.1 copy.9
Async XLA Ops:
  103.7 10.9 %copy-start = (f32[1,24,64,192]{3,2,1,0:T(8,128)S(1)}, f32[1,24,64,192]{3,2,1,0:T(8,128)}, u32[]{:S(2)}) copy-start(f32[1,24,64,192]{3,2,1,0:T(8,128)} %get-tuple-element.5) | copy-start | bytes 3538948

commit v3 on v2

--- a/solution.py
+++ b/solution.py
@@ -1,4 +1,5 @@
 import functools
+from types import SimpleNamespace
 
 import jax
 import jax.numpy as jnp
@@ -45,9 +46,33 @@
     return r * PITCH + EDGE
 
 
-def kernel(h_init, c_init, w_hbm, bias_ref, h_seq, c_last, w_ref, ws_ref, fa0, fb0, fa1, fb1, hb0, hb1, ca, cb, sb, el, er,
-           out0, out1, cio, bp, zs, to_right, to_left, from_left, from_right, diag_left, diag_right, seam,
-           w_sems, in_sems, out_sems, col_send, left_recv, right_recv, dleft_recv, dright_recv, seam_send, seam_recv):
+STATE = ("hs", "w_ref", "bp", "fa0", "fb0", "fa1", "fb1", "hb0", "ca", "cb", "zs", "el", "er")
+FIRST = ("ws_ref", "hin", "cio", "hb1", "sb", "to_right", "to_left", "from_left", "from_right", "diag_left", "diag_right", "seam")
+SEMS = ("w_sems", "in_sems", "col_send", "left_recv", "right_recv", "dleft_recv", "dright_recv", "seam_send", "seam_recv")
+
+
+def exchange_kernel(h_init, c_init, w_hbm, bias_ref, *refs):
+    names = STATE + FIRST + SEMS
+    work(True, SimpleNamespace(h_init=h_init, c_init=c_init, w_hbm=w_hbm, bias_ref=bias_ref, **dict(zip(names, refs))))
+
+
+def final_kernel(*refs):
+    outs = ("h_seq", "c_last", *["done_" + name for name in CHANGED])
+    names = STATE + outs + ("hb1", "sb", "out0", "out1", "cio", "out_sems", "in_sems")
+    work(False, SimpleNamespace(**dict(zip(names, refs))))
+
+
+CHANGED = ("fa0", "fb0", "fa1", "fb1", "hb0", "ca", "cb")
+
+
+def work(exchange, refs):
+    fa0, fb0, fa1, fb1, hb0, hb1, ca, cb = refs.fa0, refs.fb0, refs.fa1, refs.fb1, refs.hb0, refs.hb1, refs.ca, refs.cb
+    w_ref, bp, zs, el, er, sb, cio, in_sems = refs.w_ref, refs.bp, refs.zs, refs.el, refs.er, refs.sb, refs.cio, refs.in_sems
+    if exchange:
+        ws_ref, to_right, to_left, from_left, from_right = refs.ws_ref, refs.to_right, refs.to_left, refs.from_left, refs.from_right
+        diag_left, diag_right, seam = refs.diag_left, refs.diag_right, refs.seam
+    else:
+        fa0, fb0, fa1, fb1, hb0, ca, cb = (getattr(refs, "done_" + name) for name in CHANGED)
     col_count = lax.axis_size("cols")
     core = lax.axis_index("rows")
     col = lax.axis_index("cols")
@@ -58,36 +83,6 @@
     def out_row(y):
         return jnp.where(core == 0, y, ROWS - 1 - y)
 
-    in_copies = [pltpu.make_async_copy(src.at[0], dst, in_sems.at[n]) for n, (src, dst) in enumerate(((h_init, out0), (c_init, cio)))]
-    for copy in in_copies:
-        copy.start()
-    w_copies = []
-    for d in range(3):
-        kd = jnp.where(core == 0, d, 2 - d)
-        first = 4 * LANES * d
-        pieces = [(first + LANES * dx, dx, 0, LANES) for dx in range(3)] + [(first + 3 * LANES + HALF * dx, dx, LANES, HALF) for dx in range(2)]
-        for dst, dx, ch, size in pieces + [(12 * LANES + HALF * d, 2, LANES, HALF)]:
-            w_copies.append(pltpu.make_async_copy(w_hbm.at[kd, dx, pl.ds(ch, size)], ws_ref.at[pl.ds(dst, size)], w_sems.at[len(w_copies)]))
-    for copy in w_copies:
-        copy.start()
-
-    for ref in (fa0, fb0, fa1, fb1):
-        ref[0:PITCH, :] = jnp.zeros((PITCH, LANES), F32)
-        ref[(GROWS - 2) * PITCH:, :] = jnp.zeros((2 * PITCH, LANES), F32)
-    for ref in (hb0, hb1):
-        ref[0] = jnp.zeros((COLS, WIDTH), BF16)
-    ws_ref[DEPTH - HALF:, :] = jnp.zeros((HALF, GATES), BF16)
-    for ref in (el, er, from_left, from_right, diag_left, diag_right):
-        ref[...] = jnp.zeros(ref.shape, F32)
-
-    barrier = pltpu.get_barrier_semaphore()
-    pl.semaphore_signal(barrier, inc=1, device_id={"rows": other}, device_id_type=MESH)
-    for there, near in ((has_left, col - 1), (has_right, col + 1)):
-        @pl.when(there)
-        def _():
-            pl.semaphore_signal(barrier, inc=1, device_id={"cols": near}, device_id_type=MESH)
-            pl.semaphore_signal(barrier, inc=1, device_id={"cols": near, "rows": other}, device_id_type=MESH)
-
     low = lax.broadcasted_iota(jnp.int32, (1, LANES), 1) < HALF
     og_in = jnp.where(low, 0.5, 1.0).astype(F32)
     og_add = jnp.where(low, 0.5, 0.0).astype(F32)
@@ -101,23 +96,18 @@
     def gate_blocks(t):
         return [t[0], half_turn(sel(t[2], t[1])), t[3], half_turn(sel(t[5], t[4])), sel(t[1], t[2]), sel(t[4], t[5])]
 
-    for n, block in enumerate(gate_blocks([bias_ref[:, lanes(n)] for n in range(6)])):
-        bp[:, lanes(n)] = block
-
-    pl.semaphore_wait(barrier, 1 + 2 * has_left.astype(jnp.int32) + 2 * has_right.astype(jnp.int32))
-
     def side_copies(src, to, near, diag, slot, send, near_sem, diag_sem):
         return [
-            pltpu.make_async_remote_copy(src, near.at[slot], col_send.at[send], near_sem.at[slot], device_id={"cols": to}, device_id_type=MESH),
-            pltpu.make_async_remote_copy(src.at[:, pl.ds(ROWS - 8, 8)], diag.at[slot], col_send.at[send + 1], diag_sem.at[slot], device_id={"cols": to, "rows": other}, device_id_type=MESH),
+            pltpu.make_async_remote_copy(src, near.at[slot], refs.col_send.at[send], near_sem.at[slot], device_id={"cols": to}, device_id_type=MESH),
+            pltpu.make_async_remote_copy(src.at[:, pl.ds(ROWS - 8, 8)], diag.at[slot], refs.col_send.at[send + 1], diag_sem.at[slot], device_id={"cols": to, "rows": other}, device_id_type=MESH),
         ]
 
     def columns(slot, start):
         def right():
-            return side_copies(to_right, col + 1, from_left, diag_left, slot, 0, left_recv, dleft_recv)
+            return side_copies(to_right, col + 1, from_left, diag_left, slot, 0, refs.left_recv, refs.dleft_recv)
 
         def left():
-            return side_copies(to_left, col - 1, from_right, diag_right, slot, 2, right_recv, dright_recv)
+            return side_copies(to_left, col - 1, from_right, diag_right, slot, 2, refs.right_recv, refs.dright_recv)
 
         for there, copies, back in ((has_right, right, left), (has_left, left, right)):
             @pl.when(there)
@@ -131,7 +121,7 @@
     def seam_copies(slot):
         parts = [(ref, pl.ds(at_row(ROWS - k), COLS)) for k in range(2) for ref in (fa0, fb0)] + [(ref, pl.ds((ROWS - 1) * COLS, COLS)) for ref in (ca, cb)]
         return [
-            pltpu.make_async_remote_copy(ref.at[rows], seam.at[slot, n], seam_send.at[n], seam_recv.at[slot, n], device_id={"rows": other}, device_id_type=MESH)
+            pltpu.make_async_remote_copy(ref.at[rows], seam.at[slot, n], refs.seam_send.at[n], refs.seam_recv.at[slot, n], device_id={"rows": other}, device_id_type=MESH)
             for n, (ref, rows) in enumerate(parts)
         ]
 
@@ -296,40 +286,7 @@
         return [functools.partial(write_out, *state, out, y) for y in rows]
 
     def out_copy(out, t, n):
-        return pltpu.make_async_copy(out, h_seq.at[t, 0], out_sems.at[n])
-
-    for copy in in_copies:
-        copy.wait()
-
-    def load_row(y, _):
-        row = out_row(y)
-        h = out0[row].astype(F32)
-        c = cio[row]
-        to = pl.ds(pl.multiple_of(at_row(y + 1), 8), COLS)
-        cells = pl.ds(pl.multiple_of(y * COLS, COLS), COLS)
-        for a, b, where, value in ((fa0, fb0, to, h), (ca, cb, cells, c)):
-            a[where, :] = value[:, 0:LANES]
-            b[where, :] = jnp.concatenate([value[:, LANES:CH]] * 2, axis=1)
-        return 0
-
-    lax.fori_loop(0, ROWS, load_row, 0)
-    build_messages()
-
-    def load_weights(n, _):
-        rows = pl.ds(pl.multiple_of(n * HALF, HALF), HALF)
-        blocks = gate_blocks([ws_ref[rows, lanes(i)].astype(F32) for i in range(6)])
-        for i, block in enumerate(blocks):
-            w_ref[rows, lanes(i)] = block.astype(BF16)
-        return 0
-
-    for copy in w_copies:
-        copy.wait()
-    columns(0, True)
-    for copy in seam_copies(0):
-        copy.start()
-    lax.fori_loop(0, DEPTH // HALF, load_weights, 0)
-    for r in range(1, ROWS + 1):
-        assemble_inner(*old, hb0, r)
+        return pltpu.make_async_copy(out, refs.h_seq.at[t, 0], refs.out_sems.at[n])
 
     def bias_of(t):
         return bp[pl.ds(t, 1), :]
@@ -363,20 +320,14 @@
         piece(1, hb1, e_units[0], gate_tasks(0, late, bias_a, new) + edge_tasks(new, hb1, range(11, ROWS + 2)))
         piece(0, hb1, e_units[1], gate_tasks(1, e_units[0], bias_b, old) + inner_tasks(new, hb1, range(18, ROWS + 2)))
         piece(1, hb1, rows[3], gate_tasks(0, e_units[1], bias_b, old) + inner_tasks(new, hb1, range(1, 8)))
-        piece(0, hb1, rows[0], gate_tasks(1, rows[3], bias_b, old) + inner_tasks(new, hb1, range(8, 18)))
         if not last:
             build_messages()
             columns(1 - slot, True)
+        piece(0, hb1, rows[0], gate_tasks(1, rows[3], bias_b, old) + inner_tasks(new, hb1, range(8, 18)))
+        if not last:
             for copy in seam_copies(1 - slot):
                 copy.start()
-
-            @pl.when(s > 0)
-            def _():
-                for n, out in enumerate((out0, out1)):
-                    out_copy(out, 2 * s - 2 + n, n).wait()
-        else:
-            for n, out in enumerate((out0, out1)):
-                out_copy(out, 2 * s - 2 + n, n).wait()
+        out0, out1 = (refs.out0, refs.out1) if last else (refs.hs.at[2 * s], refs.hs.at[2 * s + 1])
 
         def next_operands(first, count):
             return [] if last else inner_tasks(old, hb0, range(first, first + count))
@@ -390,21 +341,94 @@
                 task()
         else:
             early(2 * s + 2, [tail, done[:6], done[6:], []])
-        for n, out in enumerate((out0, out1)):
-            out_copy(out, 2 * s + n, n).start()
-
-    early(0, [[], [], [], []])
-
-    def two_steps(s, _):
-        slot = lax.rem(s, 2)
-        halos(slot)
-        rest(s, slot, False)
-        return 0
+        if last:
+            for n, out in enumerate((out0, out1)):
+                out_copy(out, 2 * s + n, n).start()
 
     last_pair = STEPS // 2 - 1
-    lax.fori_loop(0, last_pair, two_steps, 0)
-    halos(last_pair % 2)
-    rest(last_pair, last_pair % 2, True)
+    hb1[0] = jnp.zeros((COLS, WIDTH), BF16)
+    if exchange:
+        in_copies = [pltpu.make_async_copy(src.at[0], dst, in_sems.at[n]) for n, (src, dst) in enumerate(((refs.h_init, refs.hin), (refs.c_init, cio)))]
+        for copy in in_copies:
+            copy.start()
+        w_copies = []
+        for d in range(3):
+            kd = jnp.where(core == 0, d, 2 - d)
+            first = 4 * LANES * d
+            pieces = [(first + LANES * dx, dx, 0, LANES) for dx in range(3)] + [(first + 3 * LANES + HALF * dx, dx, LANES, HALF) for dx in range(2)]
+            for dst, dx, ch, size in pieces + [(12 * LANES + HALF * d, 2, LANES, HALF)]:
+                w_copies.append(pltpu.make_async_copy(refs.w_hbm.at[kd, dx, pl.ds(ch, size)], ws_ref.at[pl.ds(dst, size)], refs.w_sems.at[len(w_copies)]))
+        for copy in w_copies:
+            copy.start()
+
+        for ref in (fa0, fb0, fa1, fb1):
+            ref[0:PITCH, :] = jnp.zeros((PITCH, LANES), F32)
+            ref[(GROWS - 2) * PITCH:, :] = jnp.zeros((2 * PITCH, LANES), F32)
+        hb0[0] = jnp.zeros((COLS, WIDTH), BF16)
+        ws_ref[DEPTH - HALF:, :] = jnp.zeros((HALF, GATES), BF16)
+        for ref in (el, er, from_left, from_right, diag_left, diag_right):
+            ref[...] = jnp.zeros(ref.shape, F32)
+
+        barrier = pltpu.get_barrier_semaphore()
+        pl.semaphore_signal(barrier, inc=1, device_id={"rows": other}, device_id_type=MESH)
+        for there, near in ((has_left, col - 1), (has_right, col + 1)):
+            @pl.when(there)
+            def _():
+                pl.semaphore_signal(barrier, inc=1, device_id={"cols": near}, device_id_type=MESH)
+                pl.semaphore_signal(barrier, inc=1, device_id={"cols": near, "rows": other}, device_id_type=MESH)
+
+        for n, block in enumerate(gate_blocks([refs.bias_ref[:, lanes(n)] for n in range(6)])):
+            bp[:, lanes(n)] = block
+
+        pl.semaphore_wait(barrier, 1 + 2 * has_left.astype(jnp.int32) + 2 * has_right.astype(jnp.int32))
+
+        for copy in in_copies:
+            copy.wait()
+
+        def load_row(y, _):
+            row = out_row(y)
+            h = refs.hin[row].astype(F32)
+            c = cio[row]
+            to = pl.ds(pl.multiple_of(at_row(y + 1), 8), COLS)
+            cells = pl.ds(pl.multiple_of(y * COLS, COLS), COLS)
+            for a, b, where, value in ((fa0, fb0, to, h), (ca, cb, cells, c)):
+                a[where, :] = value[:, 0:LANES]
+                b[where, :] = jnp.concatenate([value[:, LANES:CH]] * 2, axis=1)
+            return 0
+
+        lax.fori_loop(0, ROWS, load_row, 0)
+        build_messages()
+
+        def load_weights(n, _):
+            rows = pl.ds(pl.multiple_of(n * HALF, HALF), HALF)
+            blocks = gate_blocks([ws_ref[rows, lanes(i)].astype(F32) for i in range(6)])
+            for i, block in enumerate(blocks):
+                w_ref[rows, lanes(i)] = block.astype(BF16)
+            return 0
+
+        for copy in w_copies:
+            copy.wait()
+        columns(0, True)
+        for copy in seam_copies(0):
+            copy.start()
+        lax.fori_loop(0, DEPTH // HALF, load_weights, 0)
+        for r in range(1, ROWS + 1):
+            assemble_inner(*old, hb0, r)
+        early(0, [[], [], [], []])
+
+        def two_steps(s, _):
+            slot = lax.rem(s, 2)
+            halos(slot)
+            rest(s, slot, False)
+            return 0
+
+        lax.fori_loop(0, last_pair, two_steps, 0)
+        halos(last_pair % 2)
+        return
+
+    before = pltpu.make_async_copy(refs.hs, refs.h_seq.at[pl.ds(0, STEPS - 2), 0], refs.out_sems.at[2])
+    before.start()
+    rest(last_pair, None, True)
 
     def store_row(y, _):
         cells = pl.ds(pl.multiple_of(y * COLS, COLS), COLS)
@@ -414,9 +438,10 @@
         return 0
 
     lax.fori_loop(0, ROWS, store_row, 0)
-    c_copy = pltpu.make_async_copy(cio, c_last.at[0], in_sems.at[1])
+    c_copy = pltpu.make_async_copy(cio, refs.c_last.at[0], in_sems.at[1])
     c_copy.start()
-    for n, out in enumerate((out0, out1)):
+    before.wait()
+    for n, out in enumerate((refs.out0, refs.out1)):
         out_copy(out, STEPS - 2 + n, n).wait()
     c_copy.wait()
 
@@ -424,43 +449,61 @@
 def solution(mesh):
     def device_fn(h_init, c_init, w_rec, gate_bias):
         hbm = pl.BlockSpec(memory_space=pltpu.HBM)
+        in_vmem = pl.BlockSpec(memory_space=pltpu.VMEM)
         vmem = pltpu.VMEM
         dma = pltpu.SemaphoreType.DMA
         tile = (ROWS, COLS, CH)
         edge = (5, ROWS, LANES)
-        return pl.pallas_call(
-            kernel,
-            out_shape=(
-                jax.ShapeDtypeStruct((STEPS, 1, *tile), BF16),
-                jax.ShapeDtypeStruct((1, *tile), F32),
-            ),
-            in_specs=[hbm, hbm, hbm, pl.BlockSpec(memory_space=pltpu.VMEM)],
-            out_specs=(hbm, hbm),
+        operands = vmem((GROWS, COLS, WIDTH), BF16)
+        strips = vmem((2 * STRIP, DEPTH), BF16)
+        state = dict(
+            hs=vmem((STEPS - 2, *tile), BF16),
+            w_ref=vmem((DEPTH, GATES), BF16),
+            bp=vmem((STEPS, GATES), F32),
+            **{name: vmem((GROWS * PITCH, LANES), F32) for name in ("fa0", "fb0", "fa1", "fb1")},
+            hb0=operands,
+            **{name: vmem(((ROWS + 1) * COLS, LANES), F32) for name in ("ca", "cb")},
+            zs=vmem((len(EARLY_ROWS[3]) * INNER, GATES), F32),
+            **{name: vmem((7, EXT, LANES), F32) for name in ("el", "er")},
+        )
+        held = pl.pallas_call(
+            exchange_kernel,
+            out_shape=tuple(state[name] for name in STATE),
+            in_specs=[hbm, hbm, hbm, in_vmem],
+            out_specs=(in_vmem,) * len(STATE),
             scratch_shapes=[
-                *[vmem((DEPTH, GATES), BF16)] * 2,
-                *[vmem((GROWS * PITCH, LANES), F32)] * 4,
-                *[vmem((GROWS, COLS, WIDTH), BF16)] * 2,
-                *[vmem(((ROWS + 1) * COLS, LANES), F32)] * 2,
-                vmem((2 * STRIP, DEPTH), BF16),
-                *[vmem((7, EXT, LANES), F32)] * 2,
-                *[vmem(tile, BF16)] * 2,
+                vmem((DEPTH, GATES), BF16),
+                vmem(tile, BF16),
                 vmem(tile, F32),
-                vmem((STEPS, GATES), F32),
-                vmem((len(EARLY_ROWS[3]) * INNER, GATES), F32),
+                operands,
+                strips,
                 *[vmem(edge, F32)] * 2,
                 *[vmem((2, *edge), F32)] * 2,
                 *[vmem((2, 5, 8, LANES), F32)] * 2,
                 vmem((2, 6, COLS, LANES), F32),
                 dma((18,)),
                 dma((2,)),
-                dma((2,)),
                 dma((4,)),
                 *[dma((2,))] * 4,
                 dma((6,)),
                 dma((2, 6)),
             ],
-            compiler_params=pltpu.CompilerParams(collective_id=0, has_side_effects=True, vmem_limit_bytes=60 * 1024 * 1024),
+            compiler_params=pltpu.CompilerParams(collective_id=0, has_side_effects=True, vmem_limit_bytes=41 * 1024 * 1024),
         )(h_init, c_init, w_rec, gate_bias)
+        outs = pl.pallas_call(
+            final_kernel,
+            out_shape=(
+                jax.ShapeDtypeStruct((STEPS, 1, *tile), BF16),
+                jax.ShapeDtypeStruct((1, *tile), F32),
+                *[state[name] for name in CHANGED],
+            ),
+            in_specs=[in_vmem] * len(STATE),
+            out_specs=(hbm, hbm, *[in_vmem] * len(CHANGED)),
+            input_output_aliases={STATE.index(name): 2 + n for n, name in enumerate(CHANGED)},
+            scratch_shapes=[operands, strips, vmem(tile, BF16), vmem(tile, BF16), vmem(tile, F32), dma((3,)), dma((2,))],
+            compiler_params=pltpu.CompilerParams(vmem_limit_bytes=16 * 1024 * 1024),
+        )(*held)
+        return outs[0], outs[1]
 
     state_spec = P("dp", "rows", "cols", None)
     return jax.shard_map(device_fn, mesh=mesh, in_specs=(state_spec, state_spec, P(), P()), out_specs=(P(None, "dp", "rows", "cols", None), state_spec), check_vma=False)

time: 116 us -> 103 us (0.89)
  local copies, waits for them, and re-layouts: 12 us -> 0 us
    unnamed x4 -> x0, local copies, waits for them, and re-layouts: 12 us -> none
    pallas_call x1 -> x2, Pallas kernels: 103 us -> 102 us  [the longest x1 90.9 us: device_fn(): pl.pallas_call(exchange_kernel, out_shape=tuple((state[name] for name in...]
where the time goes in v3:
time: 103 us
  Pallas kernels  102 us (99%)
    pallas_call x1, Pallas kernels, device_fn(): pl.pallas_call(exchange_kernel, out_shape=tuple((state[name] for name in...  90.9 us
    pallas_call x1, Pallas kernels, device_fn(): pl.pallas_call(final_kernel, out_shape=(jax.ShapeDtypeStruct((STEPS, 1, *...  11.4 us

profile of v3, /device:TPU:97, one launch (start us, length us, event | category | flops | bytes accessed | tf_op | source)
XLA Modules:
  0.0 103.1 jit_solution(9594941982380973831)
XLA Ops:
  0.6 90.9 %shard_map.59 = (bf16[14,24,64,192]{3,2,1,0:T(8,128)(2,1)S(1)}, bf16[1792,768]{1,0:T(8,128)(2,1)S(1)}, f32[16,768]{1,0:T(8,128)S(1)}, f32[2160,128]{1,0:T(8,128)...) custom-call(bf16[1,24,64,192]{3,2,1,0:T(8,128)(2,1)} %h_init.1, ...), custom_call_target="tpu_custom_call" | custom-call | tf_op jit(solution)/shard_map/pallas_call | solution.py:469
  91.6 11.4 %shard_map.60 = (bf16[16,1,24,64,192]{4,3,2,1,0:T(8,128)(2,1)}, f32[1,24,64,192]{3,2,1,0:T(8,128)}, f32[2160,128]{1,0:T(8,128)S(1)}, f32[2160,128]{1,0:T(8,128)S...) custom-call(bf16[14,24,64,192]{3,2,1,0:T(8,128)(2,1)S(1)} %get-tuple, ...), custom_call_target="tpu_custom_call", output_to_operand_aliasing={{2}: (3, {}), {3}: (4, {}), {4}: (5, {}), {5}: (6, {}), {6}... | custom-call | tf_op jit(solution)/shard_map/pallas_call | solution.py:493

commit v4 on v3

--- a/solution.py
+++ b/solution.py
@@ -27,6 +27,7 @@
 WIDTH = 5 * LANES
 EXT = 2 * ROWS
 STRIP = 32
+CUTS = 4
 
 I_ROWS = [range(6 * j, 6 * j + 6) for j in range(4)]
 EARLY_ROWS = [range(6), range(6, 12), range(12, 17), range(17, 22)]
@@ -58,11 +59,16 @@
 
 def final_kernel(*refs):
     outs = ("h_seq", "c_last", *["done_" + name for name in CHANGED])
-    names = STATE + outs + ("hb1", "sb", "out0", "out1", "cio", "out_sems", "in_sems")
+    names = STATE + outs + ("hb1", "sb", "out0", "out1", "cio", "step_sems", "out_sems", "in_sems")
     work(False, SimpleNamespace(**dict(zip(names, refs))))
 
 
 CHANGED = ("fa0", "fb0", "fa1", "fb1", "hb0", "ca", "cb")
+
+
+def cut_copy(src, dst, sems):
+    size = ROWS // CUTS
+    return [pltpu.make_async_copy(src.at[pl.ds(size * k, size)], dst.at[pl.ds(size * k, size)], sems.at[k]) for k in range(CUTS)]
 
 
 def work(exchange, refs):
@@ -260,10 +266,13 @@
 
     def piece(parity, hb, units, tasks):
         lhs = jnp.concatenate([unit_lhs(hb, unit) for unit in units], axis=0)
-        half = sum(unit_rows(unit) for unit in units[:(len(units) + 1) // 2])
-        wide = [jnp.dot(lhs, w_ref[:, lanes(2 * n, 2)], preferred_element_type=F32) for n in range(2)]
-        halves = [jnp.dot(part, w_ref[:, lanes(4, 2)], preferred_element_type=F32) for part in (lhs[:half], lhs[half:])]
-        results[parity] = jnp.concatenate(wide + [jnp.concatenate(halves, axis=0)], axis=1)
+        if exchange:
+            results[parity] = jnp.dot(lhs, w_ref[...], preferred_element_type=F32)
+        else:
+            half = sum(unit_rows(unit) for unit in units[:(len(units) + 1) // 2])
+            wide = [jnp.dot(lhs, w_ref[:, lanes(2 * n, 2)], preferred_element_type=F32) for n in range(2)]
+            halves = [jnp.dot(part, w_ref[:, lanes(4, 2)], preferred_element_type=F32) for part in (lhs[:half], lhs[half:])]
+            results[parity] = jnp.concatenate(wide + [jnp.concatenate(halves, axis=0)], axis=1)
         for task in tasks:
             task()
 
@@ -286,7 +295,7 @@
         return [functools.partial(write_out, *state, out, y) for y in rows]
 
     def out_copy(out, t, n):
-        return pltpu.make_async_copy(out, refs.h_seq.at[t, 0], refs.out_sems.at[n])
+        return cut_copy(out, refs.h_seq.at[t, 0], refs.out_sems.at[n])
 
     def bias_of(t):
         return bp[pl.ds(t, 1), :]
@@ -337,18 +346,19 @@
         tail = gate_tasks(0, rows[2], bias_b, old) + next_operands(13, 6)
         done = out_tasks(old, out1, I_ROWS[1]) + out_tasks(old, out1, I_ROWS[2])
         if last:
+            for copy in out_copy(out0, 2 * s, 0):
+                copy.start()
             for task in tail + done:
                 task()
+            for copy in out_copy(out1, 2 * s + 1, 1):
+                copy.start()
         else:
             early(2 * s + 2, [tail, done[:6], done[6:], []])
-        if last:
-            for n, out in enumerate((out0, out1)):
-                out_copy(out, 2 * s + n, n).start()
 
     last_pair = STEPS // 2 - 1
     hb1[0] = jnp.zeros((COLS, WIDTH), BF16)
     if exchange:
-        in_copies = [pltpu.make_async_copy(src.at[0], dst, in_sems.at[n]) for n, (src, dst) in enumerate(((refs.h_init, refs.hin), (refs.c_init, cio)))]
+        in_copies = cut_copy(refs.h_init.at[0], refs.hin, in_sems.at[0]) + cut_copy(refs.c_init.at[0], cio, in_sems.at[1])
         for copy in in_copies:
             copy.start()
         w_copies = []
@@ -380,38 +390,38 @@
         for n, block in enumerate(gate_blocks([refs.bias_ref[:, lanes(n)] for n in range(6)])):
             bp[:, lanes(n)] = block
 
-        pl.semaphore_wait(barrier, 1 + 2 * has_left.astype(jnp.int32) + 2 * has_right.astype(jnp.int32))
 
         for copy in in_copies:
             copy.wait()
 
-        def load_row(y, _):
-            row = out_row(y)
-            h = refs.hin[row].astype(F32)
-            c = cio[row]
-            to = pl.ds(pl.multiple_of(at_row(y + 1), 8), COLS)
-            cells = pl.ds(pl.multiple_of(y * COLS, COLS), COLS)
-            for a, b, where, value in ((fa0, fb0, to, h), (ca, cb, cells, c)):
-                a[where, :] = value[:, 0:LANES]
-                b[where, :] = jnp.concatenate([value[:, LANES:CH]] * 2, axis=1)
+        def load_rows(n, _):
+            for k in range(4):
+                y = 4 * n + k
+                row = out_row(y)
+                to = pl.ds(pl.multiple_of(at_row(y + 1), 8), COLS)
+                cells = pl.ds(pl.multiple_of(y * COLS, COLS), COLS)
+                for a, b, where, value in ((fa0, fb0, to, refs.hin[row].astype(F32)), (ca, cb, cells, cio[row])):
+                    a[where, :] = value[:, 0:LANES]
+                    b[where, :] = jnp.concatenate([value[:, LANES:CH]] * 2, axis=1)
             return 0
 
-        lax.fori_loop(0, ROWS, load_row, 0)
+        lax.fori_loop(0, ROWS // 4, load_rows, 0)
         build_messages()
 
         def load_weights(n, _):
-            rows = pl.ds(pl.multiple_of(n * HALF, HALF), HALF)
+            rows = pl.ds(pl.multiple_of(n * 4 * HALF, HALF), 4 * HALF)
             blocks = gate_blocks([ws_ref[rows, lanes(i)].astype(F32) for i in range(6)])
             for i, block in enumerate(blocks):
                 w_ref[rows, lanes(i)] = block.astype(BF16)
             return 0
 
-        for copy in w_copies:
-            copy.wait()
+        pl.semaphore_wait(barrier, 1 + 2 * has_left.astype(jnp.int32) + 2 * has_right.astype(jnp.int32))
         columns(0, True)
         for copy in seam_copies(0):
             copy.start()
-        lax.fori_loop(0, DEPTH // HALF, load_weights, 0)
+        for copy in w_copies:
+            copy.wait()
+        lax.fori_loop(0, DEPTH // HALF // 4, load_weights, 0)
         for r in range(1, ROWS + 1):
             assemble_inner(*old, hb0, r)
         early(0, [[], [], [], []])
@@ -426,8 +436,9 @@
         halos(last_pair % 2)
         return
 
-    before = pltpu.make_async_copy(refs.hs, refs.h_seq.at[pl.ds(0, STEPS - 2), 0], refs.out_sems.at[2])
-    before.start()
+    before = [pltpu.make_async_copy(refs.hs.at[t], refs.h_seq.at[t, 0], refs.step_sems.at[t]) for t in range(STEPS - 2)]
+    for copy in before:
+        copy.start()
     rest(last_pair, None, True)
 
     def store_row(y, _):
@@ -438,12 +449,11 @@
         return 0
 
     lax.fori_loop(0, ROWS, store_row, 0)
-    c_copy = pltpu.make_async_copy(cio, refs.c_last.at[0], in_sems.at[1])
-    c_copy.start()
-    before.wait()
-    for n, out in enumerate((refs.out0, refs.out1)):
-        out_copy(out, STEPS - 2 + n, n).wait()
-    c_copy.wait()
+    c_copies = cut_copy(cio, refs.c_last.at[0], in_sems.at[0])
+    for copy in c_copies:
+        copy.start()
+    for copy in before + out_copy(refs.out0, STEPS - 2, 0) + out_copy(refs.out1, STEPS - 1, 1) + c_copies:
+        copy.wait()
 
 
 def solution(mesh):
@@ -482,7 +492,7 @@
                 *[vmem((2, 5, 8, LANES), F32)] * 2,
                 vmem((2, 6, COLS, LANES), F32),
                 dma((18,)),
-                dma((2,)),
+                dma((2, CUTS)),
                 dma((4,)),
                 *[dma((2,))] * 4,
                 dma((6,)),
@@ -500,7 +510,7 @@
             in_specs=[in_vmem] * len(STATE),
             out_specs=(hbm, hbm, *[in_vmem] * len(CHANGED)),
             input_output_aliases={STATE.index(name): 2 + n for n, name in enumerate(CHANGED)},
-            scratch_shapes=[operands, strips, vmem(tile, BF16), vmem(tile, BF16), vmem(tile, F32), dma((3,)), dma((2,))],
+            scratch_shapes=[operands, strips, vmem(tile, BF16), vmem(tile, BF16), vmem(tile, F32), dma((STEPS - 2,)), dma((2, CUTS)), dma((1, CUTS))],
             compiler_params=pltpu.CompilerParams(vmem_limit_bytes=16 * 1024 * 1024),
         )(*held)
         return outs[0], outs[1]

time: 103 us -> 100 us (0.971)
  Pallas kernels: 102 us -> 99.5 us
    pallas_call x1, Pallas kernels: 90.9 us -> 88.1 us  [device_fn(): pl.pallas_call(exchange_kernel, out_shape=tuple((state[name] for name in...]
where the time goes in v4:
time: 100 us
  Pallas kernels  99.5 us (100%)
    pallas_call x1, Pallas kernels, device_fn(): pl.pallas_call(exchange_kernel, out_shape=tuple((state[name] for name in...  88.1 us
    pallas_call x1, Pallas kernels, device_fn(): pl.pallas_call(final_kernel, out_shape=(jax.ShapeDtypeStruct((STEPS, 1, *...  11.3 us

profile of v4, /device:TPU:97, one launch (start us, length us, event | category | flops | bytes accessed | tf_op | source)
XLA Modules:
  0.0 100.3 jit_solution(403615317106261548)
XLA Ops:
  0.6 88.1 %shard_map.59 = (bf16[14,24,64,192]{3,2,1,0:T(8,128)(2,1)S(1)}, bf16[1792,768]{1,0:T(8,128)(2,1)S(1)}, f32[16,768]{1,0:T(8,128)S(1)}, f32[2160,128]{1,0:T(8,128)...) custom-call(bf16[1,24,64,192]{3,2,1,0:T(8,128)(2,1)} %h_init.1, ...), custom_call_target="tpu_custom_call" | custom-call | tf_op jit(solution)/shard_map/pallas_call | solution.py:479
  88.8 11.3 %shard_map.60 = (bf16[16,1,24,64,192]{4,3,2,1,0:T(8,128)(2,1)}, f32[1,24,64,192]{3,2,1,0:T(8,128)}, f32[2160,128]{1,0:T(8,128)S(1)}, f32[2160,128]{1,0:T(8,128)S...) custom-call(bf16[14,24,64,192]{3,2,1,0:T(8,128)(2,1)S(1)} %get-tuple, ...), custom_call_target="tpu_custom_call", output_to_operand_aliasing={{2}: (3, {}), {3}: (4, {}), {4}: (5, {}), {5}: (6, {}), {6}... | custom-call | tf_op jit(solution)/shard_map/pallas_call | solution.py:503

commit v5 on v4

--- a/solution.py
+++ b/solution.py
@@ -264,9 +264,9 @@
     old, new = (fa0, fb0), (fa1, fb1)
     results = [None, None]
 
-    def piece(parity, hb, units, tasks):
+    def piece(parity, hb, units, tasks, cut=not exchange):
         lhs = jnp.concatenate([unit_lhs(hb, unit) for unit in units], axis=0)
-        if exchange:
+        if not cut:
             results[parity] = jnp.dot(lhs, w_ref[...], preferred_element_type=F32)
         else:
             half = sum(unit_rows(unit) for unit in units[:(len(units) + 1) // 2])
@@ -332,7 +332,7 @@
         if not last:
             build_messages()
             columns(1 - slot, True)
-        piece(0, hb1, rows[0], gate_tasks(1, rows[3], bias_b, old) + inner_tasks(new, hb1, range(8, 18)))
+        piece(0, hb1, rows[0], gate_tasks(1, rows[3], bias_b, old) + inner_tasks(new, hb1, range(8, 18)), True)
         if not last:
             for copy in seam_copies(1 - slot):
                 copy.start()

time: 100 us -> 101 us (1.010)
  no operation moved by 1% of the time
where the time goes in v5:
time: 101 us
  Pallas kernels  99.8 us (99%)
    pallas_call x1, Pallas kernels, device_fn(): pl.pallas_call(exchange_kernel, out_shape=tuple((state[name] for name in...  88.5 us
    pallas_call x1, Pallas kernels, device_fn(): pl.pallas_call(final_kernel, out_shape=(jax.ShapeDtypeStruct((STEPS, 1, *...  11.3 us

profile of v5, /device:TPU:97, one launch (start us, length us, event | category | flops | bytes accessed | tf_op | source)
XLA Modules:
  0.0 100.6 jit_solution(14170071594497103373)
XLA Ops:
  0.6 88.5 %shard_map.59 = (bf16[14,24,64,192]{3,2,1,0:T(8,128)(2,1)S(1)}, bf16[1792,768]{1,0:T(8,128)(2,1)S(1)}, f32[16,768]{1,0:T(8,128)S(1)}, f32[2160,128]{1,0:T(8,128)...) custom-call(bf16[1,24,64,192]{3,2,1,0:T(8,128)(2,1)} %h_init.1, ...), custom_call_target="tpu_custom_call" | custom-call | tf_op jit(solution)/shard_map/pallas_call | solution.py:479
  89.1 11.3 %shard_map.60 = (bf16[16,1,24,64,192]{4,3,2,1,0:T(8,128)(2,1)}, f32[1,24,64,192]{3,2,1,0:T(8,128)}, f32[2160,128]{1,0:T(8,128)S(1)}, f32[2160,128]{1,0:T(8,128)S...) custom-call(bf16[14,24,64,192]{3,2,1,0:T(8,128)(2,1)S(1)} %get-tuple, ...), custom_call_target="tpu_custom_call", output_to_operand_aliasing={{2}: (3, {}), {3}: (4, {}), {4}: (5, {}), {5}: (6, {}), {6}... | custom-call | tf_op jit(solution)/shard_map/pallas_call | solution.py:503
